TPU v7x, 32 devices: a 4x4x1 block of a 4x4x8 slice. The times are simulated.
32 devices in a mesh: data: 1 (over z), pp: 4 (over y), ep: 8 (over x, core).
Axes of the slice: x: 4, y: 4, z: 1, core: 2. Of those that a mesh axis runs over, the one named last changes fastest.
The devices are a block of a 4x4x8 slice.
Arguments:
- expert_out: bfloat16 [4, 64, 256, 3584], P(('data', 'pp'), 'ep')
- expert_ids: int32 [4, 8, 192, 8], P(('data', 'pp'), 'ep')
- slot_ids: int32 [4, 8, 192, 8], P(('data', 'pp'), 'ep')
- gate_vals: float32 [4, 8, 192, 8], P(('data', 'pp'), 'ep')
- residual: bfloat16 [4, 8, 192, 3584], P(('data', 'pp'), 'ep')
- norm_scale: float32 [4, 3584], P('pp')
- w_query: bfloat16 [4, 3584, 28, 128], P('pp')
- w_key: bfloat16 [4, 3584, 28, 128], P('pp')
- w_value: bfloat16 [4, 3584, 28, 128], P('pp')
- w_out: bfloat16 [4, 28, 128, 3584], P('pp')
Outputs:
- output: bfloat16 [4, 8, 192, 3584], P(('data', 'pp'), 'ep')
All inputs are finite; a program needn't handle non-finite values.
Results may differ from a plain program's by a relative error of at most 0.02.
Values are sent between devices in bfloat16 or wider.
A program may use at most 768 MiB of HBM per device.

v0:
```python
import jax
import jax.numpy as jnp
from jax import lax
from jax.sharding import PartitionSpec as P

NORM_EPS = 1e-6


def attn_block(merged, scale_vec, w_query, w_key, w_value, w_out):
    head_dim = w_query.shape[-1]
    seq_len = merged.shape[1]
    resid_f32 = merged.astype(jnp.float32)
    inv_rms = lax.rsqrt(jnp.mean(resid_f32 * resid_f32, axis=-1, keepdims=True) + NORM_EPS)
    normed_in = (resid_f32 * inv_rms * scale_vec).astype(jnp.bfloat16)
    q_heads = jnp.einsum('bld,dhe->blhe', normed_in, w_query, preferred_element_type=jnp.float32).astype(jnp.bfloat16)
    k_heads = jnp.einsum('bld,dhe->blhe', normed_in, w_key, preferred_element_type=jnp.float32).astype(jnp.bfloat16)
    v_heads = jnp.einsum('bld,dhe->blhe', normed_in, w_value, preferred_element_type=jnp.float32).astype(jnp.bfloat16)
    scores = jnp.einsum('bqhe,bkhe->bhqk', q_heads, k_heads, preferred_element_type=jnp.float32) * (head_dim ** -0.5)
    causal = jnp.arange(seq_len)[:, None] >= jnp.arange(seq_len)[None, :]
    scores = jnp.where(causal, scores, -1e30)
    exp_scores = jnp.exp(scores - jnp.max(scores, axis=-1, keepdims=True))
    row_sums = jnp.sum(exp_scores, axis=-1)
    mixed_vals = jnp.einsum('bhqk,bkhe->bqhe', exp_scores.astype(jnp.bfloat16), v_heads, preferred_element_type=jnp.float32)
    attn_out = (mixed_vals / jnp.swapaxes(row_sums, -1, -2)[..., None]).astype(jnp.bfloat16)
    proj_out = jnp.einsum('crif,ife->cre', attn_out, w_out, preferred_element_type=jnp.float32).astype(jnp.bfloat16)
    return (resid_f32 + proj_out.astype(jnp.float32)).astype(jnp.bfloat16)


def solution(mesh):
    ep_size = mesh.shape['ep']
    pp_size = mesh.shape['pp']
    next_stage = [(source, (source + 1) % pp_size) for source in range(pp_size)]
    token_spec = P(('data', 'pp'), 'ep', None, None)
    weight_spec = P('pp', None, None, None)

    def body(expert_out, expert_ids, slot_ids, gate_vals, residual, norm_scale, w_query, w_key, w_value, w_out):
        local_experts, capacity, model_width = expert_out.shape[1:]
        cap_dev = capacity // ep_size
        send_buf = expert_out[0].reshape(local_experts, ep_size, cap_dev, model_width)
        received = lax.all_to_all(send_buf, 'ep', 1, 0, tiled=True).reshape(-1, model_width)
        kept_mask = slot_ids[0] >= 0
        local_slot = slot_ids[0] - lax.axis_index('ep') * cap_dev
        row_ids = jnp.where(kept_mask, expert_ids[0] * cap_dev + local_slot, 0)
        gate_used = jnp.where(kept_mask, gate_vals[0], 0.0)
        picked_rows = jnp.take(received, row_ids, axis=0)
        merged = (residual[0].astype(jnp.float32) + jnp.sum(picked_rows * gate_used[..., None], axis=-2)).astype(jnp.bfloat16)
        arrived = lax.ppermute(merged, 'pp', next_stage)
        result = attn_block(arrived, norm_scale[0], w_query[0], w_key[0], w_value[0], w_out[0])
        return result[None]

    return jax.shard_map(body, mesh=mesh, in_specs=(token_spec, token_spec, token_spec, token_spec, token_spec, P('pp', None), weight_spec, weight_spec, weight_spec, weight_spec), out_specs=token_spec, check_vma=False)
```

profile of v0, /device:TPU:97, one launch (start us, length us, event | category | flops | bytes accessed | tf_op | source)
XLA Modules:
  0.0 327.6 jit_solution(15045965581788067708)
XLA Ops:
  0.0 13.5 %copy.16 = bf16[8,8,32,3584]{3,2,0,1:T(8,128)(2,1)} copy(bf16[8,8,32,3584]{3,2,1,0:T(8,128)(2,1)} %bitcast.118) | data formatting | bytes 29360128 | tf_op jit(solution)/shard_map/reshape;squeeze | solution.py:39
  13.5 0.0 copy-start.1
  13.5 0.0 copy-start.2
  13.5 0.0 copy-start.4
  13.5 7.6 %all-to-all-start = ((bf16[8,8,32,3584]{3,2,0,1:T(8,128)(2,1)}), bf16[8,8,32,3584]{3,2,0,1:T(8,128)(2,1)}, u32[]{:S(2)}, u32[]{:S(2)}) async-start(bf16[8,8,32,3584]{3,2,0,1:T(8,128)(2,1)} %copy.16), calls=%async_computation | async-start | bytes 29360128 | tf_op jit(solution)/shard_map/all_to_all | solution.py:40
  21.1 0.0 copy-done.1
  21.1 0.0 copy-done.2
  21.1 0.1 copy.17
  21.2 0.1 reshape.236
  21.4 0.0 copy-done.4
  21.4 0.1 copy.18
  21.5 0.1 copy.15
  21.7 160.5 %all-to-all-done = bf16[8,8,32,3584]{3,2,0,1:T(8,128)(2,1)} async-done(((bf16[8,8,32,3584]{3,2,0,1:T(8,128)(2,1)}), bf16[8,8,32,3584]{3,2,0,1:T(8,128)(2,1)}, u32[]{:S(2)}, u32[]{:S(2)}) %all-to-all-start) | async-done | bytes 14680096 | tf_op jit(solution)/shard_map/all_to_all | solution.py:40
  182.1 27.3 %gather_fusion = bf16[1536,3584]{1,0:T(8,128)(2,1)} fusion(bf16[2048,3584]{1,0:T(8,128)(2,1)} %bitcast.5, s32[2048]{0:T(1024)S(1)} %pad_clamp_fusion), kind=kCustom, calls=%fused_computation | custom fusion | bytes 22026240 | tf_op jit(solution)/shard_map/jit(_take)/gather | solution.py:45
  209.4 0.0 copy-start
  209.4 26.5 %multiply_reduce_fusion = f32[192,3584]{1,0:T(8,128)S(1)} fusion(bf16[1536,3584]{1,0:T(8,128)(2,1)} %gather_fusion, f32[192,8]{1,0:T(8,128)S(1)} %copy.18, pred[192,8]{1,0:T(8,128)(4,1)S(1)} %copy.15), kind=kLoop, calls=%fused_computation.9 | loop fusion | flops 21331968 | bytes 13770240 | tf_op jit(solution)/shard_map/reduce_sum | solution.py:46
  236.0 0.0 copy-done
  236.0 0.0 copy-start.3
  236.0 0.3 fusion.38
  236.3 1.5 collective-permute-start
  237.8 0.0 copy-done.3
  237.8 32.0 %collective-permute-done = bf16[1,192,3584]{2,1,0:T(8,128)(2,1)S(1)} collective-permute-done((bf16[1,192,3584]{2,1,0:T(8,128)(2,1)S(1)}, bf16[1,192,3584]{2,1,0:T(8,128)(2,1)S(1)}, u32[]{:S(2)}, u32[]{:S(2)}) %collective-permute-start) | collective-permute-done | bytes 1376288 | tf_op jit(solution)/shard_map/ppermute | solution.py:47
  269.8 0.4 fusion.32
  270.2 11.3 %fusion.46 = bf16[192,28,128]{2,0,1:T(8,128)(2,1)S(1)} fusion(bf16[1,3584,28,128]{3,1,2,0:T(8,128)(2,1)} %param.16, bf16[1,192,3584]{2,1,0:T(8,128)(2,1)S(1)} %collective-permute-done, f32[3584]{0:T(1024)S(1)} %reduce.6, f32[192]{0:T(256)S(1)} %add_rsqrt_fusion), kind=kOutput, calls=%fused_computation.38 | convolution fusion | flops 4935942144 | bytes 28457728 | tf_op jit(solution)/shard_map/bld,dhe->blhe/dot_general | solution.py:15
  281.5 13.1 %fusion.14 = (f32[28,192]{1,0:T(8,128)S(1)}, f32[28,192,192]{1,2,0:T(8,128)}) fusion(pred[192,192]{0,1:T(8,128)(4,1)S(1)} %iota_compare_fusion, bf16[192,28,128]{2,0,1:T(8,128)(2,1)S(1)} %fusion.46, bf16[1,3584,28,128]{3,1,2,0:T(8,128)(2,1)} %param.17, bf16[1,192,3584]{2,1,0:T(8,128)(2,1)S(1)} %collective-permute-done, f32[3584]{0:T(1024)S(1)} %reduce.6, ...), kind=kOutput, calls=%fused_computation.15 | convolution fusion | flops 5203274752 | bytes 32644864 | tf_op jit(solution)/shard_map/bqhe,bkhe->bhqk/dot_general | solution.py:18
  294.6 3.9 %fusion.30 = f32[28,192]{1,0:T(8,128)S(1)} fusion(f32[28,192,192]{1,2,0:T(8,128)} %get-tuple-element.6, f32[28,192]{1,0:T(8,128)S(1)} %get-tuple-element.5, pred[192,192]{0,1:T(8,128)(4,1)S(1)} %iota_compare_fusion), kind=kLoop, calls=%fused_computation.21 | loop fusion | flops 4123392 | bytes 4208640 | tf_op jit(solution)/shard_map/reduce_sum | solution.py:22
  298.5 11.5 %fusion.43 = bf16[192,28,128]{2,0,1:T(8,128)(2,1)S(1)} fusion(bf16[1,3584,28,128]{3,1,2,0:T(8,128)(2,1)} %param.18, bf16[1,192,3584]{2,1,0:T(8,128)(2,1)S(1)} %collective-permute-done, f32[3584]{0:T(1024)S(1)} %reduce.6, f32[192]{0:T(256)S(1)} %add_rsqrt_fusion), kind=kOutput, calls=%fused_computation.37 | convolution fusion | flops 4935942144 | bytes 28457728 | tf_op jit(solution)/shard_map/bld,dhe->blhe/dot_general | solution.py:17
  310.0 17.6 %fusion.27 = bf16[1,1,192,3584]{3,2,1,0:T(8,128)(2,1)} fusion(bf16[1,28,128,3584]{3,2,1,0:T(8,128)(2,1)} %param.19, bf16[1,192,3584]{2,1,0:T(8,128)(2,1)S(1)} %collective-permute-done, f32[192,28]{0,1:T(8,128)S(1)} %bitcast.119, bf16[192,28,128]{2,0,1:T(8,128)(2,1)S(1)} %fusion.43, f32[28,192,192]{1,2,0:T(8,128)} %get-tuple-element.6, ...), kind=kOutput, calls=%fused_computation.20 | convolution fusion | flops 5205688320 | bytes 34027520 | tf_op jit(solution)/shard_map/crif,ife->cre/dot_general | solution.py:25
  (7 shorter events, 0.1 us)
Async XLA Ops:
  13.5 7.6 %copy-start.1 = (s32[1,1,192,8]{2,3,1,0:T(8,128)S(1)}, s32[1,1,192,8]{2,3,1,0:T(8,128)}, u32[]{:S(2)}) copy-start(s32[1,1,192,8]{2,3,1,0:T(8,128)} %param.12) | copy-start | bytes 18436
  13.5 7.6 %copy-start.2 = (s32[1,1,192,8]{2,3,1,0:T(8,128)S(1)}, s32[1,1,192,8]{2,3,1,0:T(8,128)}, u32[]{:S(2)}) copy-start(s32[1,1,192,8]{2,3,1,0:T(8,128)} %param.11) | copy-start | bytes 18436
  13.5 7.9 %copy-start.4 = (f32[1,1,192,8]{2,3,1,0:T(8,128)S(1)}, f32[1,1,192,8]{2,3,1,0:T(8,128)}, u32[]{:S(2)}) copy-start(f32[1,1,192,8]{2,3,1,0:T(8,128)} %param.13) | copy-start | bytes 18436
  13.5 168.6 %all-to-all-start = ((bf16[8,8,32,3584]{3,2,0,1:T(8,128)(2,1)}), bf16[8,8,32,3584]{3,2,0,1:T(8,128)(2,1)}, u32[]{:S(2)}, u32[]{:S(2)}) async-start(bf16[8,8,32,3584]{3,2,0,1:T(8,128)(2,1)} %copy.16), calls=%async_computation | async-start | bytes 29360128 | tf_op jit(solution)/shard_map/all_to_all | solution.py:40
  209.4 26.5 %copy-start = (bf16[1,1,192,3584]{3,2,1,0:T(8,128)(2,1)S(1)}, bf16[1,1,192,3584]{3,2,1,0:T(8,128)(2,1)}, u32[]{:S(2)}) copy-start(bf16[1,1,192,3584]{3,2,1,0:T(8,128)(2,1)} %param.14) | copy-start | bytes 4128772
  236.0 1.8 copy-start.3
  236.3 33.5 %collective-permute-start = (bf16[1,192,3584]{2,1,0:T(8,128)(2,1)S(1)}, bf16[1,192,3584]{2,1,0:T(8,128)(2,1)S(1)}, u32[]{:S(2)}, u32[]{:S(2)}) collective-permute-start(bf16[1,192,3584]{2,1,0:T(8,128)(2,1)S(1)} %fusion.38), channel_id=1, source_target_pairs={{0,8},{8,16},{16,24},{24,0},{1,9},{9,17},{17,25},{25,1},{2,10},{10... | collective-permute-start | bytes 4128776 | tf_op jit(solution)/shard_map/ppermute | solution.py:47
where the time goes:
time: 328 us
  waiting for transfers between devices  192 us (59%)
  matrix products  53.6 us (16%)
  local copies, waits for them, and re-layouts  41.3 us (13%)
  other arithmetic  31.1 us (9%)
  starting transfers between devices  9.12 us (3%)
    all_to_all x1, waiting for transfers between devices, body(): lax.all_to_all(send_buf, 'ep', 1, 0, tiled=True).reshape(-1, model_width)  160 us
    ppermute x1, waiting for transfers between devices, body(): arrived = lax.ppermute(merged, 'pp', next_stage)  32 us
    gather x1, local copies, waits for them, and re-layouts, body(): picked_rows = jnp.take(received, row_ids, axis=0)  27.3 us
    reduce_sum x1, other arithmetic, body(): jnp.sum(picked_rows * gate_used[..., None], axis=-2)  26.5 us
    dot_general x1, matrix products, attn_block(): jnp.einsum('crif,ife->cre', attn_out, w_out, preferred_element_type=jnp.f...  17.6 us
    another operation x1, local copies, waits for them, and re-layouts, body(): expert_out[0].reshape(local_experts, ep_size, cap_dev, model_width)  13.5 us
    dot_general x1, matrix products, attn_block(): jnp.einsum('bqhe,bkhe->bhqk', q_heads, k_heads, preferred_element_type=jn...  13.1 us
    dot_general x1, matrix products, attn_block(): jnp.einsum('bld,dhe->blhe', normed_in, w_value, preferred_element_type=jn...  11.5 us
  transfers between devices with their start and end apart: 2, of which 2 were waited for; matrix products, arithmetic and copies ran while one was open for 0% of the time, Pallas kernels for 0%

commit v1 on v0

--- a/solution.py
+++ b/solution.py
@@ -1,9 +1,15 @@
+import functools
+
 import jax
 import jax.numpy as jnp
 from jax import lax
+from jax.experimental import pallas as pl
+from jax.experimental.pallas import tpu as pltpu
 from jax.sharding import PartitionSpec as P
 
 NORM_EPS = 1e-6
+COLS = 256
+MESH = pl.DeviceIdType.MESH
 
 
 def attn_block(merged, scale_vec, w_query, w_key, w_value, w_out):
@@ -26,26 +32,223 @@
     return (resid_f32 + proj_out.astype(jnp.float32)).astype(jnp.bfloat16)
 
 
+def combine_kernel(sizes, o_hbm, ids, slots, gates, h_hbm, y_out,
+                   rows_v, resid_v, meta, gate_mats, send_v, recv_v, ysend_v, y_v,
+                   rows_loc, rows_ss, rows_rs, res_loc, res_ss, res_rs, meta_ss, meta_rs,
+                   ring_ss, ring_rs, y_ss, y_rs, out_sem):
+    ep, pp, experts, cap, width, tokens, top = sizes
+    chips = ep // 2
+    half = width // 2
+    blocks = half // COLS
+    cap_dev = cap // ep
+    chip_rows = 2 * experts * cap_dev
+    me = lax.axis_index('ep')
+    stage = lax.axis_index('pp')
+    chip, core = me // 2, me % 2
+    partner = chip * 2 + (1 - core)
+    ahead, behind, across = (chip + 1) % chips, (chip + chips - 1) % chips, (chip + 2) % chips
+    next_stage, prev_stage = (stage + 1) % pp, (stage + pp - 1) % pp
+    right, left = 2 * ahead + core, 2 * behind + core
+    owners = (2 * across, 2 * across + 1, 2 * ahead + 1, 2 * behind, 2 * ahead, 2 * behind + 1, 2 * chip, 2 * chip + 1)
+
+    def local_rows(j):
+        cols = pl.ds(pl.multiple_of(core * half + j * COLS, COLS), COLS)
+        return pltpu.make_async_copy(o_hbm.at[:, :, cols], rows_v.at[j, pl.ds(core * experts, experts)], rows_loc.at[j])
+
+    def swap_rows(j):
+        cols = pl.ds(pl.multiple_of((1 - core) * half + j * COLS, COLS), COLS)
+        return pltpu.make_async_remote_copy(
+            src_ref=o_hbm.at[:, :, cols], dst_ref=rows_v.at[j, pl.ds(core * experts, experts)],
+            send_sem=rows_ss.at[j], recv_sem=rows_rs.at[j], device_id={'ep': partner}, device_id_type=MESH)
+
+    own_cols = pl.ds(pl.multiple_of(core * half, COLS), half)
+    other_cols = pl.ds(pl.multiple_of((1 - core) * half, COLS), half)
+    local_resid = pltpu.make_async_copy(h_hbm.at[:, own_cols], resid_v.at[core], res_loc)
+    swap_resid = pltpu.make_async_remote_copy(
+        src_ref=h_hbm.at[:, other_cols], dst_ref=resid_v.at[core],
+        send_sem=res_ss, recv_sem=res_rs, device_id={'ep': partner}, device_id_type=MESH)
+
+    def meta_copy(step):
+        return pltpu.make_async_remote_copy(
+            src_ref=meta.at[me], dst_ref=meta.at[me], send_sem=meta_ss.at[step - 1], recv_sem=meta_rs.at[step - 1],
+            device_id={'ep': (me + step) % ep}, device_id_type=MESH)
+
+    def ring_copy(kind, j):
+        target = right if kind % 2 == 0 else left
+        return pltpu.make_async_remote_copy(
+            src_ref=send_v.at[kind, j % 2], dst_ref=recv_v.at[kind, j], send_sem=ring_ss.at[kind, j],
+            recv_sem=ring_rs.at[kind, j], device_id={'ep': target}, device_id_type=MESH)
+
+    def y_copy(side, j):
+        return pltpu.make_async_remote_copy(
+            src_ref=ysend_v.at[side, j % 2], dst_ref=y_v.at[core * blocks + j], send_sem=y_ss.at[side, j],
+            recv_sem=y_rs.at[core * blocks + j], device_id={'pp': next_stage, 'ep': 2 * chip + side}, device_id_type=MESH)
+
+    for j in range(blocks):
+        local_rows(j).start()
+    local_resid.start()
+    row_ids = jnp.where(slots[...] >= 0, ids[...] * cap_dev + slots[...] - me * cap_dev, -1)
+    meta[me, 0:top, :] = row_ids.astype(jnp.float32)
+    meta[me, top:2 * top, :] = gates[...]
+
+    barrier = pltpu.get_barrier_semaphore()
+    for step in range(1, ep):
+        pl.semaphore_signal(barrier, inc=1, device_id={'ep': (me + step) % ep}, device_id_type=MESH)
+    for side in range(2):
+        pl.semaphore_signal(barrier, inc=1, device_id={'pp': next_stage, 'ep': 2 * chip + side}, device_id_type=MESH)
+        pl.semaphore_signal(barrier, inc=1, device_id={'pp': prev_stage, 'ep': 2 * chip + side}, device_id_type=MESH)
+    pl.semaphore_wait(barrier, ep - 1 + 4)
+
+    for step in range(1, ep):
+        meta_copy(step).start()
+    for j in range(blocks):
+        swap_rows(j).start()
+    swap_resid.start()
+
+    def build_gates(role):
+        table = jnp.transpose(meta[owners[role]])
+        wanted = (lax.broadcasted_iota(jnp.int32, (tokens, chip_rows), 1) + chip * chip_rows).astype(jnp.float32)
+        total = jnp.zeros((tokens, chip_rows), jnp.float32)
+        for t in range(top):
+            total = total + jnp.where(table[:, t:t + 1] == wanted, table[:, top + t:top + t + 1], 0.0)
+        high = total.astype(jnp.bfloat16)
+        rest = total - high.astype(jnp.float32)
+        mid = rest.astype(jnp.bfloat16)
+        low = (rest - mid.astype(jnp.float32)).astype(jnp.bfloat16)
+        gate_mats[role, 0:tokens] = high
+        gate_mats[role, tokens:2 * tokens] = mid
+        gate_mats[role, 2 * tokens:3 * tokens] = low
+
+    def contribution(role, j):
+        slot0 = pl.multiple_of(owners[role] * cap_dev, cap_dev)
+        rows = rows_v[j, :, pl.ds(slot0, cap_dev), :].reshape(chip_rows, COLS)
+        parts = jnp.dot(gate_mats[role], rows, preferred_element_type=jnp.float32)
+        return parts[2 * tokens:] + parts[tokens:2 * tokens] + parts[:tokens]
+
+    def finish(j):
+        for side, (near, far) in enumerate(((3, 4), (2, 5))):
+            own = contribution(6 + side, j)
+
+            @pl.when(j >= 2)
+            def _():
+                y_copy(side, j - 2).wait_send()
+
+            ring_copy(near, j).wait_recv()
+            ring_copy(far, j).wait_recv()
+            cols = pl.ds(pl.multiple_of(j * COLS, COLS), COLS)
+            total = resid_v[side, :, cols].astype(jnp.float32) + (own + recv_v[near, j] + recv_v[far, j])
+            ysend_v[side, j % 2] = total.astype(jnp.bfloat16)
+            y_copy(side, j).start()
+
+    for step in range(1, ep):
+        meta_copy(step).wait_recv()
+
+    def block_step(j, carry):
+        local_rows(j).wait()
+        swap_rows(j).wait_recv()
+
+        for kind in range(4):
+            @pl.when(j == 0)
+            def _():
+                build_gates(kind)
+
+            @pl.when(j >= 2)
+            def _():
+                ring_copy(kind, j - 2).wait_send()
+
+            send_v[kind, j % 2] = contribution(kind, j)
+            ring_copy(kind, j).start()
+
+        @pl.when(j == 0)
+        def _():
+            for role in range(4, 8):
+                build_gates(role)
+            local_resid.wait()
+            swap_resid.wait_recv()
+
+        @pl.when(j > 0)
+        def _():
+            finish(j - 1)
+
+        for kind in (4, 5):
+            own = contribution(kind, j)
+
+            @pl.when(j >= 2)
+            def _():
+                ring_copy(kind, j - 2).wait_send()
+
+            ring_copy(kind - 4, j).wait_recv()
+            send_v[kind, j % 2] = own + recv_v[kind - 4, j]
+            ring_copy(kind, j).start()
+        return carry
+
+    lax.fori_loop(0, blocks, block_step, 0)
+    finish(blocks - 1)
+
+    def y_arrived(i):
+        pltpu.make_async_copy(y_v.at[i], y_v.at[i], y_rs.at[i]).wait()
+
+    def store_out(i):
+        return pltpu.make_async_copy(y_v.at[i], y_out.at[:, pl.ds(i * COLS, COLS)], out_sem.at[i])
+
+    for j in range(blocks):
+        for side in range(2):
+            i = side * blocks + j
+            y_arrived(i)
+            store_out(i).start()
+    for i in range(2 * blocks):
+        store_out(i).wait()
+    for step in range(1, ep):
+        meta_copy(step).wait_send()
+    for j in range(blocks):
+        swap_rows(j).wait_send()
+    swap_resid.wait_send()
+    for j in range(blocks - 2, blocks):
+        for kind in range(6):
+            ring_copy(kind, j).wait_send()
+        for side in range(2):
+            y_copy(side, j).wait_send()
+
+
+def combine_and_send(ep, pp, expert_out, expert_ids, slot_ids, gate_vals, residual):
+    experts, cap, width = expert_out.shape
+    tokens, top = expert_ids.shape
+    sizes = (ep, pp, experts, cap, width, tokens, top)
+    blocks = width // 2 // COLS
+    chip_rows = 2 * experts * cap // ep
+    any_spec = pl.BlockSpec(memory_space=pl.ANY)
+    vmem_spec = pl.BlockSpec(memory_space=pltpu.VMEM)
+    dma = pltpu.SemaphoreType.DMA
+    return pl.pallas_call(
+        functools.partial(combine_kernel, sizes),
+        out_shape=jax.ShapeDtypeStruct((tokens, width), jnp.bfloat16),
+        in_specs=[any_spec, vmem_spec, vmem_spec, vmem_spec, any_spec],
+        out_specs=any_spec,
+        scratch_shapes=[
+            pltpu.VMEM((blocks, 2 * experts, cap, COLS), jnp.bfloat16),
+            pltpu.VMEM((2, tokens, width // 2), jnp.bfloat16),
+            pltpu.VMEM((ep, 2 * top, tokens), jnp.float32),
+            pltpu.VMEM((8, 3 * tokens, chip_rows), jnp.bfloat16),
+            pltpu.VMEM((6, 2, tokens, COLS), jnp.float32),
+            pltpu.VMEM((6, blocks, tokens, COLS), jnp.float32),
+            pltpu.VMEM((2, 2, tokens, COLS), jnp.bfloat16),
+            pltpu.VMEM((2 * blocks, tokens, COLS), jnp.bfloat16),
+            dma((blocks,)), dma((blocks,)), dma((blocks,)), dma, dma, dma, dma((ep - 1,)), dma((ep - 1,)),
+            dma((6, blocks)), dma((6, blocks)), dma((2, blocks)), dma((2 * blocks,)), dma((2 * blocks,)),
+        ],
+        compiler_params=pltpu.CompilerParams(collective_id=0, has_side_effects=True, vmem_limit_bytes=60 * 2 ** 20),
+    )(expert_out, expert_ids.T, slot_ids.T, gate_vals.T, residual)
+
+
 def solution(mesh):
     ep_size = mesh.shape['ep']
     pp_size = mesh.shape['pp']
-    next_stage = [(source, (source + 1) % pp_size) for source in range(pp_size)]
     token_spec = P(('data', 'pp'), 'ep', None, None)
     weight_spec = P('pp', None, None, None)
 
     def body(expert_out, expert_ids, slot_ids, gate_vals, residual, norm_scale, w_query, w_key, w_value, w_out):
-        local_experts, capacity, model_width = expert_out.shape[1:]
-        cap_dev = capacity // ep_size
-        send_buf = expert_out[0].reshape(local_experts, ep_size, cap_dev, model_width)
-        received = lax.all_to_all(send_buf, 'ep', 1, 0, tiled=True).reshape(-1, model_width)
-        kept_mask = slot_ids[0] >= 0
-        local_slot = slot_ids[0] - lax.axis_index('ep') * cap_dev
-        row_ids = jnp.where(kept_mask, expert_ids[0] * cap_dev + local_slot, 0)
-        gate_used = jnp.where(kept_mask, gate_vals[0], 0.0)
-        picked_rows = jnp.take(received, row_ids, axis=0)
-        merged = (residual[0].astype(jnp.float32) + jnp.sum(picked_rows * gate_used[..., None], axis=-2)).astype(jnp.bfloat16)
-        arrived = lax.ppermute(merged, 'pp', next_stage)
-        result = attn_block(arrived, norm_scale[0], w_query[0], w_key[0], w_value[0], w_out[0])
+        arrived = combine_and_send(ep_size, pp_size, expert_out[0], expert_ids[0, 0], slot_ids[0, 0], gate_vals[0, 0], residual[0, 0])
+        result = attn_block(arrived[None], norm_scale[0], w_query[0], w_key[0], w_value[0], w_out[0])
         return result[None]
 
     return jax.shard_map(body, mesh=mesh, in_specs=(token_spec, token_spec, token_spec, token_spec, token_spec, P('pp', None), weight_spec, weight_spec, weight_spec, weight_spec), out_specs=token_spec, check_vma=False)

time: 328 us -> 172 us (0.52)
  waiting for transfers between devices: 192 us -> 0 us
  Pallas kernels: 0 us -> 113 us
  local copies, waits for them, and re-layouts: 41.3 us -> 0.01 us
  other arithmetic: 31.1 us -> 5.67 us
  starting transfers between devices: 9.12 us -> 0 us
    all_to_all x1 -> x0, waiting for transfers between devices: 160 us -> none  [body(): lax.all_to_all(send_buf, 'ep', 1, 0, tiled=True).reshape(-1, model_width)]
    pallas_call x0 -> x1, Pallas kernels: none -> 113 us  [combine_and_send(): pl.pallas_call(functools.partial(combine_kernel, sizes), out_shape=jax.Sh...]
    ppermute x1 -> x0, waiting for transfers between devices: 32 us -> none  [body(): arrived = lax.ppermute(merged, 'pp', next_stage)]
    gather x1 -> x0, local copies, waits for them, and re-layouts: 27.3 us -> none  [body(): picked_rows = jnp.take(received, row_ids, axis=0)]
    reduce_sum x1 -> x0, other arithmetic: 26.5 us -> none  [body(): jnp.sum(picked_rows * gate_used[..., None], axis=-2)]
    another operation x1 -> x0, local copies, waits for them, and re-layouts: 13.5 us -> none  [body(): expert_out[0].reshape(local_experts, ep_size, cap_dev, model_width)]
    all_to_all x1 -> x0, starting transfers between devices: 7.61 us -> none  [body(): lax.all_to_all(send_buf, 'ep', 1, 0, tiled=True).reshape(-1, model_width)]
  transfers between devices with their start and end apart: 2 -> 0, of which waited for: 2 -> 0; matrix products, arithmetic and copies ran while one was open for 0% -> 0% of each run, Pallas kernels for 0% -> 0%
where the time goes in v1:
time: 172 us
  Pallas kernels  113 us (66%)
  matrix products  53.9 us (31%)
  other arithmetic  5.67 us (3%)
    pallas_call x1, Pallas kernels, combine_and_send(): pl.pallas_call(functools.partial(combine_kernel, sizes), out_shape=jax.Sh...  113 us
    dot_general x1, matrix products, attn_block(): jnp.einsum('crif,ife->cre', attn_out, w_out, preferred_element_type=jnp.f...  17.7 us
    dot_general x1, matrix products, attn_block(): jnp.einsum('bqhe,bkhe->bhqk', q_heads, k_heads, preferred_element_type=jn...  13.3 us
    dot_general x1, matrix products, attn_block(): jnp.einsum('bld,dhe->blhe', normed_in, w_query, preferred_element_type=jn...  11.5 us
    dot_general x1, matrix products, attn_block(): jnp.einsum('bld,dhe->blhe', normed_in, w_value, preferred_element_type=jn...  11.3 us
    reduce_sum x1, other arithmetic, attn_block(): row_sums = jnp.sum(exp_scores, axis=-1)  3.91 us

profile of v1, /device:TPU:97, one launch (start us, length us, event | category | flops | bytes accessed | tf_op | source)
XLA Modules:
  0.0 172.2 jit_solution(3145809224950184605)
XLA Ops:
  0.0 0.0 copy-start.1
  0.0 112.6 %shard_map.100 = bf16[192,3584]{1,0:T(8,128)(2,1)} custom-call(bf16[8,256,3584]{2,1,0:T(8,128)(2,1)} %bitcast.86, s32[8,192]{1,0:T(8,128)} %bitcast.89, s32[8,192]{1,0:T(8,128)} %bitcast.90, f32[8,192]{1,0:T(8,128)} %bitcast.91, bf16[192,3584]{1,0:T(8,128)(2,1)} %bitcast.87), custom_call_target="tpu_custom_call" | custom-call | tf_op jit(solution)/shard_map/pallas_call | solution.py:222
  112.6 1.7 fusion.29
  114.3 0.0 copy-done.1
  114.3 0.0 copy-start
  114.3 11.5 %fusion.42 = bf16[192,28,128]{2,0,1:T(8,128)(2,1)S(1)} fusion(bf16[1,3584,28,128]{3,1,2,0:T(8,128)(2,1)} %param.16, bf16[192,3584]{1,0:T(8,128)(2,1)} %shard_map.100, f32[3584]{0:T(1024)S(1)} %reduce.6, f32[192]{0:T(256)S(1)} %add_rsqrt_fusion), kind=kOutput, calls=%fused_computation.32 | convolution fusion | flops 4935942144 | bytes 28457728 | tf_op jit(solution)/shard_map/bld,dhe->blhe/dot_general | solution.py:21
  125.9 0.0 copy-done
  125.9 13.3 %fusion.23 = (f32[28,192]{1,0:T(8,128)S(1)}, f32[28,192,192]{1,2,0:T(8,128)}) fusion(pred[192,192]{0,1:T(8,128)(4,1)S(1)} %iota_compare_fusion, bf16[192,28,128]{2,0,1:T(8,128)(2,1)S(1)} %fusion.42, bf16[1,3584,28,128]{3,1,2,0:T(8,128)(2,1)} %param.17, bf16[192,3584]{1,0:T(8,128)(2,1)S(1)} %copy-done, f32[3584]{0:T(1024)S(1)} %reduce.6, ...), kind=kOutput, calls=%fused_computation.15 | convolution fusion | flops 5203274752 | bytes 32644864 | tf_op jit(solution)/shard_map/bqhe,bkhe->bhqk/dot_general | solution.py:24
  139.3 3.9 %fusion.27 = f32[28,192]{1,0:T(8,128)S(1)} fusion(f32[28,192,192]{1,2,0:T(8,128)} %get-tuple-element.6, f32[28,192]{1,0:T(8,128)S(1)} %get-tuple-element.5, pred[192,192]{0,1:T(8,128)(4,1)S(1)} %iota_compare_fusion), kind=kLoop, calls=%fused_computation.17 | loop fusion | flops 4123392 | bytes 4208640 | tf_op jit(solution)/shard_map/reduce_sum | solution.py:28
  143.2 11.3 %fusion.39 = bf16[192,28,128]{2,0,1:T(8,128)(2,1)S(1)} fusion(bf16[1,3584,28,128]{3,1,2,0:T(8,128)(2,1)} %param.18, bf16[192,3584]{1,0:T(8,128)(2,1)S(1)} %copy-done, f32[3584]{0:T(1024)S(1)} %reduce.6, f32[192]{0:T(256)S(1)} %add_rsqrt_fusion), kind=kOutput, calls=%fused_computation.31 | convolution fusion | flops 4935942144 | bytes 28457728 | tf_op jit(solution)/shard_map/bld,dhe->blhe/dot_general | solution.py:23
  154.5 17.7 %fusion.24 = bf16[1,1,192,3584]{3,2,1,0:T(8,128)(2,1)} fusion(bf16[1,28,128,3584]{3,2,1,0:T(8,128)(2,1)} %param.19, bf16[192,3584]{1,0:T(8,128)(2,1)S(1)} %copy-done, f32[192,28]{0,1:T(8,128)S(1)} %bitcast.88, bf16[192,28,128]{2,0,1:T(8,128)(2,1)S(1)} %fusion.39, f32[28,192,192]{1,2,0:T(8,128)} %get-tuple-element.6, f32[28,192]{1,0:T(8,128)S(1)} %get-tuple-element.5, ...), kind=kOutput, calls=%fused_computation.16 | convolution fusion | flops 5205688320 | bytes 34027520 | tf_op jit(solution)/shard_map/crif,ife->cre/dot_general | solution.py:31
  (3 shorter events, 0.1 us)
Async XLA Ops:
  0.0 114.3 %copy-start.1 = (f32[1,3584]{1,0:T(1,128)S(1)}, f32[1,3584]{1,0:T(1,128)}, u32[]{:S(2)}) copy-start(f32[1,3584]{1,0:T(1,128)} %param.15) | copy-start | bytes 43012
  114.3 11.6 %copy-start = (bf16[192,3584]{1,0:T(8,128)(2,1)S(1)}, bf16[192,3584]{1,0:T(8,128)(2,1)}, u32[]{:S(2)}) copy-start(bf16[192,3584]{1,0:T(8,128)(2,1)} %shard_map.100) | copy-start | bytes 4128772

commit v2 on v1

--- a/solution.py
+++ b/solution.py
@@ -9,34 +9,15 @@
 
 NORM_EPS = 1e-6
 COLS = 256
+SLOTS = 19
 MESH = pl.DeviceIdType.MESH
 
 
-def attn_block(merged, scale_vec, w_query, w_key, w_value, w_out):
-    head_dim = w_query.shape[-1]
-    seq_len = merged.shape[1]
-    resid_f32 = merged.astype(jnp.float32)
-    inv_rms = lax.rsqrt(jnp.mean(resid_f32 * resid_f32, axis=-1, keepdims=True) + NORM_EPS)
-    normed_in = (resid_f32 * inv_rms * scale_vec).astype(jnp.bfloat16)
-    q_heads = jnp.einsum('bld,dhe->blhe', normed_in, w_query, preferred_element_type=jnp.float32).astype(jnp.bfloat16)
-    k_heads = jnp.einsum('bld,dhe->blhe', normed_in, w_key, preferred_element_type=jnp.float32).astype(jnp.bfloat16)
-    v_heads = jnp.einsum('bld,dhe->blhe', normed_in, w_value, preferred_element_type=jnp.float32).astype(jnp.bfloat16)
-    scores = jnp.einsum('bqhe,bkhe->bhqk', q_heads, k_heads, preferred_element_type=jnp.float32) * (head_dim ** -0.5)
-    causal = jnp.arange(seq_len)[:, None] >= jnp.arange(seq_len)[None, :]
-    scores = jnp.where(causal, scores, -1e30)
-    exp_scores = jnp.exp(scores - jnp.max(scores, axis=-1, keepdims=True))
-    row_sums = jnp.sum(exp_scores, axis=-1)
-    mixed_vals = jnp.einsum('bhqk,bkhe->bqhe', exp_scores.astype(jnp.bfloat16), v_heads, preferred_element_type=jnp.float32)
-    attn_out = (mixed_vals / jnp.swapaxes(row_sums, -1, -2)[..., None]).astype(jnp.bfloat16)
-    proj_out = jnp.einsum('crif,ife->cre', attn_out, w_out, preferred_element_type=jnp.float32).astype(jnp.bfloat16)
-    return (resid_f32 + proj_out.astype(jnp.float32)).astype(jnp.bfloat16)
-
-
-def combine_kernel(sizes, o_hbm, ids, slots, gates, h_hbm, y_out,
-                   rows_v, resid_v, meta, gate_mats, send_v, recv_v, ysend_v, y_v,
-                   rows_loc, rows_ss, rows_rs, res_loc, res_ss, res_rs, meta_ss, meta_rs,
-                   ring_ss, ring_rs, y_ss, y_rs, out_sem):
-    ep, pp, experts, cap, width, tokens, top = sizes
+def layer_kernel(sizes, o_hbm, ids, slots, gates, h_hbm, scale_ref, wq_hbm, wk_hbm, wv_hbm, wo_hbm, z_out,
+                 pool, resid_v, meta, gate_mats, send_v, recv_v, ysend_v, y_v, square_v, x_v, qkv_v, mix_v, z_v,
+                 rows_loc, rows_ss, rows_rs, res_loc, res_ss, res_rs, meta_ss, meta_rs,
+                 ring_ss, ring_rs, y_ss, y_rs, w_sem, z_sem):
+    ep, pp, experts, cap, width, tokens, top, heads, head_dim = sizes
     chips = ep // 2
     half = width // 2
     blocks = half // COLS
@@ -53,12 +34,12 @@
 
     def local_rows(j):
         cols = pl.ds(pl.multiple_of(core * half + j * COLS, COLS), COLS)
-        return pltpu.make_async_copy(o_hbm.at[:, :, cols], rows_v.at[j, pl.ds(core * experts, experts)], rows_loc.at[j])
+        return pltpu.make_async_copy(o_hbm.at[:, :, cols], pool.at[j, pl.ds(core * experts, experts)], rows_loc.at[j])
 
     def swap_rows(j):
         cols = pl.ds(pl.multiple_of((1 - core) * half + j * COLS, COLS), COLS)
         return pltpu.make_async_remote_copy(
-            src_ref=o_hbm.at[:, :, cols], dst_ref=rows_v.at[j, pl.ds(core * experts, experts)],
+            src_ref=o_hbm.at[:, :, cols], dst_ref=pool.at[j, pl.ds(core * experts, experts)],
             send_sem=rows_ss.at[j], recv_sem=rows_rs.at[j], device_id={'ep': partner}, device_id_type=MESH)
 
     own_cols = pl.ds(pl.multiple_of(core * half, COLS), half)
@@ -84,9 +65,59 @@
             src_ref=ysend_v.at[side, j % 2], dst_ref=y_v.at[core * blocks + j], send_sem=y_ss.at[side, j],
             recv_sem=y_rs.at[core * blocks + j], device_id={'pp': next_stage, 'ep': 2 * chip + side}, device_id_type=MESH)
 
+
+    pairs = heads // 2
+    depth = width // COLS
+    n_slots = pool.shape[0]
+    early = n_slots - blocks
+    units = 3 * pairs + width // COLS
+
+    def qkv_copies(which, pair, slot):
+        w_hbm = (wq_hbm, wk_hbm, wv_hbm)[which]
+        return [pltpu.make_async_copy(w_hbm.at[2 * pair + i], pool.at[slot, 0:depth, :, i * head_dim:(i + 1) * head_dim],
+                                      w_sem.at[slot, i]) for i in range(2)]
+
+    def out_copies(n, slot):
+        cols = pl.ds(pl.multiple_of(n * COLS, COLS), COLS)
+        mid = depth // 2
+        return [pltpu.make_async_copy(wo_hbm.at[i * mid:(i + 1) * mid, :, cols], pool.at[slot, i * mid:(i + 1) * mid],
+                                      w_sem.at[slot, i]) for i in range(2)]
+
+    def slot_of(unit):
+        return (unit + blocks) % n_slots
+
+    def start_all(copies):
+        for copy in copies:
+            copy.start()
+
+    def start_unit(unit, which):
+        @pl.when(unit < 3 * pairs)
+        def _():
+            start_all(qkv_copies(which, unit // 3, slot_of(unit)))
+
+        @pl.when(jnp.logical_and(unit >= 3 * pairs, unit < units))
+        def _():
+            start_all(out_copies(unit - 3 * pairs, slot_of(unit)))
+
+    def start_any(unit):
+        for which in range(3):
+            @pl.when(unit % 3 == which)
+            def _():
+                start_unit(unit, which)
+
+    def square_piece(j):
+        for side in range(2):
+            piece = y_v[side * blocks + j].astype(jnp.float32)
+            square_v[...] += piece * piece
+
+    def wait_y(j):
+        for side in range(2):
+            pltpu.make_async_copy(y_v.at[side * blocks + j], y_v.at[side * blocks + j], y_rs.at[side * blocks + j]).wait()
+
     for j in range(blocks):
         local_rows(j).start()
     local_resid.start()
+    square_v[...] = jnp.zeros_like(square_v)
     row_ids = jnp.where(slots[...] >= 0, ids[...] * cap_dev + slots[...] - me * cap_dev, -1)
     meta[me, 0:top, :] = row_ids.astype(jnp.float32)
     meta[me, top:2 * top, :] = gates[...]
@@ -121,7 +152,7 @@
 
     def contribution(role, j):
         slot0 = pl.multiple_of(owners[role] * cap_dev, cap_dev)
-        rows = rows_v[j, :, pl.ds(slot0, cap_dev), :].reshape(chip_rows, COLS)
+        rows = pool[j, :, pl.ds(slot0, cap_dev), :].reshape(chip_rows, COLS)
         parts = jnp.dot(gate_mats[role], rows, preferred_element_type=jnp.float32)
         return parts[2 * tokens:] + parts[tokens:2 * tokens] + parts[:tokens]
 
@@ -165,10 +196,18 @@
                 build_gates(role)
             local_resid.wait()
             swap_resid.wait_recv()
+            for unit in range(early):
+                start_all(qkv_copies(unit % 3, unit // 3, slot_of(unit)))
 
         @pl.when(j > 0)
         def _():
             finish(j - 1)
+            start_any(early + j - 1)
+
+        @pl.when(j > 1)
+        def _():
+            wait_y(j - 2)
+            square_piece(j - 2)
 
         for kind in (4, 5):
             own = contribution(kind, j)
@@ -185,19 +224,88 @@
     lax.fori_loop(0, blocks, block_step, 0)
     finish(blocks - 1)
 
-    def y_arrived(i):
-        pltpu.make_async_copy(y_v.at[i], y_v.at[i], y_rs.at[i]).wait()
-
-    def store_out(i):
-        return pltpu.make_async_copy(y_v.at[i], y_out.at[:, pl.ds(i * COLS, COLS)], out_sem.at[i])
-
-    for j in range(blocks):
-        for side in range(2):
-            i = side * blocks + j
-            y_arrived(i)
-            store_out(i).start()
-    for i in range(2 * blocks):
-        store_out(i).wait()
+    start_any(early + blocks - 1)
+    for j in (blocks - 2, blocks - 1):
+        wait_y(j)
+        square_piece(j)
+    mean = jnp.sum(square_v[...], axis=-1, keepdims=True) / width
+    inv_rms = lax.rsqrt(mean + NORM_EPS)
+    for i in range(depth):
+        cols = slice(i * COLS, (i + 1) * COLS)
+        x_v[:, cols] = (y_v[i].astype(jnp.float32) * inv_rms * scale_ref[:, cols]).astype(jnp.bfloat16)
+
+    def wait_unit(unit):
+        for copy in out_copies(0, slot_of(unit)):
+            copy.wait()
+
+    def weight(unit):
+        return pool[slot_of(unit), 0:depth].reshape(width, COLS)
+
+    def project(pair):
+        for which in range(3):
+            product = jnp.dot(x_v[...], weight(3 * pair + which), preferred_element_type=jnp.float32)
+            qkv_v[pair % 2, which] = product.astype(jnp.bfloat16)
+
+    causal = lax.broadcasted_iota(jnp.int32, (tokens, tokens), 0) >= lax.broadcasted_iota(jnp.int32, (tokens, tokens), 1)
+
+    def attend(pair):
+        mixed = []
+        for i in range(2):
+            lanes = slice(i * head_dim, (i + 1) * head_dim)
+            q, k, v = (qkv_v[pair % 2, which, :, lanes] for which in range(3))
+            scores = lax.dot_general(q, k, (((1,), (1,)), ((), ())), preferred_element_type=jnp.float32) * head_dim ** -0.5
+            scores = jnp.where(causal, scores, -1e30)
+            exps = jnp.exp(scores - jnp.max(scores, axis=-1, keepdims=True))
+            sums = jnp.sum(exps, axis=-1, keepdims=True)
+            mixed.append((jnp.dot(exps.astype(jnp.bfloat16), v, preferred_element_type=jnp.float32) / sums).astype(jnp.bfloat16))
+        return mixed
+
+    def store_mixed(pair, mixed):
+        for i in range(2):
+            mix_v[:, pl.ds(pl.multiple_of(pair * COLS + i * head_dim, head_dim), head_dim)] = mixed[i]
+
+    def refill(pair):
+        for which in range(3):
+            start_unit(3 * pair + which + n_slots, (which + n_slots) % 3)
+
+    def wait_pair(pair):
+        for which in range(3):
+            wait_unit(3 * pair + which)
+
+    wait_pair(0)
+    project(0)
+    refill(0)
+
+    def pair_step(pair, carry):
+        wait_pair(pair)
+        mixed = attend(pair - 1)
+        project(pair)
+        store_mixed(pair - 1, mixed)
+        refill(pair)
+        return carry
+
+    lax.fori_loop(1, pairs, pair_step, 0)
+    store_mixed(pairs - 1, attend(pairs - 1))
+
+    def store_z(n):
+        return pltpu.make_async_copy(z_v.at[n % 2], z_out.at[:, pl.ds(pl.multiple_of(n * COLS, COLS), COLS)], z_sem.at[n % 2])
+
+    def out_step(n, carry):
+        wait_unit(3 * pairs + n)
+        product = jnp.dot(mix_v[...], weight(3 * pairs + n), preferred_element_type=jnp.float32).astype(jnp.bfloat16)
+
+        @pl.when(n >= 2)
+        def _():
+            store_z(n - 2).wait()
+
+        z_v[n % 2] = (y_v[n].astype(jnp.float32) + product.astype(jnp.float32)).astype(jnp.bfloat16)
+        store_z(n).start()
+        start_unit(3 * pairs + n + n_slots, 0)
+        return carry
+
+    lax.fori_loop(0, depth, out_step, 0)
+    store_z(depth - 2).wait()
+    store_z(depth - 1).wait()
     for step in range(1, ep):
         meta_copy(step).wait_send()
     for j in range(blocks):
@@ -210,22 +318,28 @@
             y_copy(side, j).wait_send()
 
 
-def combine_and_send(ep, pp, expert_out, expert_ids, slot_ids, gate_vals, residual):
+def combine_and_attend(ep, pp, expert_out, expert_ids, slot_ids, gate_vals, residual, norm_scale, w_query, w_key, w_value, w_out):
     experts, cap, width = expert_out.shape
     tokens, top = expert_ids.shape
-    sizes = (ep, pp, experts, cap, width, tokens, top)
+    heads, head_dim = w_query.shape[1:]
+    sizes = (ep, pp, experts, cap, width, tokens, top, heads, head_dim)
     blocks = width // 2 // COLS
+    depth = width // COLS
     chip_rows = 2 * experts * cap // ep
     any_spec = pl.BlockSpec(memory_space=pl.ANY)
     vmem_spec = pl.BlockSpec(memory_space=pltpu.VMEM)
     dma = pltpu.SemaphoreType.DMA
+
+    def by_head(weights):
+        return jnp.swapaxes(weights, 0, 1).reshape(heads, depth, COLS, head_dim)
+
     return pl.pallas_call(
-        functools.partial(combine_kernel, sizes),
+        functools.partial(layer_kernel, sizes),
         out_shape=jax.ShapeDtypeStruct((tokens, width), jnp.bfloat16),
-        in_specs=[any_spec, vmem_spec, vmem_spec, vmem_spec, any_spec],
+        in_specs=[any_spec, vmem_spec, vmem_spec, vmem_spec, any_spec, vmem_spec] + [any_spec] * 4,
         out_specs=any_spec,
         scratch_shapes=[
-            pltpu.VMEM((blocks, 2 * experts, cap, COLS), jnp.bfloat16),
+            pltpu.VMEM((SLOTS, 2 * experts, cap, COLS), jnp.bfloat16),
             pltpu.VMEM((2, tokens, width // 2), jnp.bfloat16),
             pltpu.VMEM((ep, 2 * top, tokens), jnp.float32),
             pltpu.VMEM((8, 3 * tokens, chip_rows), jnp.bfloat16),
@@ -233,11 +347,17 @@
             pltpu.VMEM((6, blocks, tokens, COLS), jnp.float32),
             pltpu.VMEM((2, 2, tokens, COLS), jnp.bfloat16),
             pltpu.VMEM((2 * blocks, tokens, COLS), jnp.bfloat16),
+            pltpu.VMEM((tokens, COLS), jnp.float32),
+            pltpu.VMEM((tokens, width), jnp.bfloat16),
+            pltpu.VMEM((2, 3, tokens, COLS), jnp.bfloat16),
+            pltpu.VMEM((tokens, heads * head_dim), jnp.bfloat16),
+            pltpu.VMEM((2, tokens, COLS), jnp.bfloat16),
             dma((blocks,)), dma((blocks,)), dma((blocks,)), dma, dma, dma, dma((ep - 1,)), dma((ep - 1,)),
-            dma((6, blocks)), dma((6, blocks)), dma((2, blocks)), dma((2 * blocks,)), dma((2 * blocks,)),
+            dma((6, blocks)), dma((6, blocks)), dma((2, blocks)), dma((2 * blocks,)), dma((SLOTS, 2)), dma((2,)),
         ],
-        compiler_params=pltpu.CompilerParams(collective_id=0, has_side_effects=True, vmem_limit_bytes=60 * 2 ** 20),
-    )(expert_out, expert_ids.T, slot_ids.T, gate_vals.T, residual)
+        compiler_params=pltpu.CompilerParams(collective_id=0, has_side_effects=True, vmem_limit_bytes=67043328),
+    )(expert_out, expert_ids.T, slot_ids.T, gate_vals.T, residual, norm_scale[None],
+      by_head(w_query), by_head(w_key), by_head(w_value), w_out.reshape(heads * head_dim // COLS, COLS, width))
 
 
 def solution(mesh):
@@ -247,8 +367,9 @@
     weight_spec = P('pp', None, None, None)
 
     def body(expert_out, expert_ids, slot_ids, gate_vals, residual, norm_scale, w_query, w_key, w_value, w_out):
-        arrived = combine_and_send(ep_size, pp_size, expert_out[0], expert_ids[0, 0], slot_ids[0, 0], gate_vals[0, 0], residual[0, 0])
-        result = attn_block(arrived[None], norm_scale[0], w_query[0], w_key[0], w_value[0], w_out[0])
-        return result[None]
+        result = combine_and_attend(
+            ep_size, pp_size, expert_out[0], expert_ids[0, 0], slot_ids[0, 0], gate_vals[0, 0], residual[0, 0],
+            norm_scale[0], w_query[0], w_key[0], w_value[0], w_out[0])
+        return result[None, None]
 
     return jax.shard_map(body, mesh=mesh, in_specs=(token_spec, token_spec, token_spec, token_spec, token_spec, P('pp', None), weight_spec, weight_spec, weight_spec, weight_spec), out_specs=token_spec, check_vma=False)

time: 172 us -> 147 us (0.85)
  matrix products: 53.9 us -> 0 us
  Pallas kernels: 113 us -> 144 us
  other arithmetic: 5.67 us -> 0 us
  local copies, waits for them, and re-layouts: 0.01 us -> 2.51 us
    dot_general x4 -> x0, matrix products: 53.9 us -> none  [the longest x1 17.7 us: attn_block(): jnp.einsum('crif,ife->cre', attn_out, w_out, preferred_element_type=jnp.f...]
    pallas_call x1, Pallas kernels: 113 us -> 144 us  [combine_and_attend(): pl.pallas_call(functools.partial(layer_kernel, sizes), out_shape=jax.Shap...]
    reduce_sum x2 -> x0, other arithmetic: 5.6 us -> none  [the longest x1 3.91 us: attn_block(): row_sums = jnp.sum(exp_scores, axis=-1)]
    unnamed x4 -> x1, local copies, waits for them, and re-layouts: 0.01 us -> 2.51 us
where the time goes in v2:
time: 147 us
  Pallas kernels  144 us (98%)
  local copies, waits for them, and re-layouts  2.51 us (2%)
    pallas_call x1, Pallas kernels, combine_and_attend(): pl.pallas_call(functools.partial(layer_kernel, sizes), out_shape=jax.Shap...  144 us

profile of v2, /device:TPU:97, one launch (start us, length us, event | category | flops | bytes accessed | tf_op | source)
XLA Modules:
  0.0 146.6 jit_solution(6894586708938493081)
XLA Ops:
  0.0 144.1 %shard_map.100 = bf16[192,3584]{1,0:T(8,128)(2,1)} custom-call(bf16[8,256,3584]{2,1,0:T(8,128)(2,1)} %bitcast.32, s32[8,192]{1,0:T(8,128)} %bitcast.35, s32[8,192]{1,0:T(8,128)} %bitcast.36, f32[8,192]{1,0:T(8,128)} %bitcast.37, bf16[192,3584]{1,0:T(8,128)(2,1)} %bitcast.34, f32[1,3584]{1,0:T(1,128)} %scale_ref.1, bf16[28,14,256,128]{3,2,1,0:T(8,128)(2,1)} %bitcast.28, ...), custom_call_target="tpu_custom_call" | custom-call | tf_op jit(solution)/shard_map/pallas_call | solution.py:336
  144.1 2.5 %copy.12 = bf16[1,1,192,3584]{3,2,1,0:T(8,128)(2,1)} copy(bf16[1,1,192,3584]{3,2,1,0:T(8,128)(2,1)} %bitcast.33) | data formatting | bytes 2752512

commit v3 on v1

v3 whole, which is shorter than its diff:
```python
import functools

import jax
import jax.numpy as jnp
from jax import lax
from jax.experimental import pallas as pl
from jax.experimental.pallas import tpu as pltpu
from jax.sharding import PartitionSpec as P

NORM_EPS = 1e-6
COLS = 256
CHUNK = 96
RING_SLOTS = 10
MESH = pl.DeviceIdType.MESH


def layer_kernel(sizes, o_hbm, ids, slots, gates, h_hbm, scale_ref, wq_hbm, wk_hbm, wv_hbm, wo_hbm, z_out,
                 pool, resid_v, meta, gate_mats, send_v, recv_v, ysend_v, y_v, square_v, x_v, q_v, kv_v, mix_v, z_v,
                 rows_loc, rows_ss, rows_rs, res_loc, res_ss, res_rs, meta_ss, meta_rs,
                 ring_ss, ring_rs, y_ss, y_rs, relay_ss, relay_rs, mix_ss, mix_rs, w_sem, z_sem, zr_ss, zr_rs):
    ep, pp, experts, cap, width, tokens, top, heads, head_dim = sizes
    chips = ep // 2
    half = width // 2
    blocks = half // COLS
    chunks = tokens // CHUNK
    steps = chunks * blocks
    depth = width // COLS
    pairs = heads // 4
    cap_dev = cap // ep
    chip_rows = 2 * experts * cap_dev
    units = chunks * pairs * 3
    me = lax.axis_index('ep')
    stage = lax.axis_index('pp')
    chip, core = me // 2, me % 2
    partner = chip * 2 + (1 - core)
    ahead, behind, across = (chip + 1) % chips, (chip + chips - 1) % chips, (chip + 2) % chips
    next_stage, prev_stage = (stage + 1) % pp, (stage + pp - 1) % pp
    right, left = 2 * ahead + core, 2 * behind + core
    owners = (2 * across, 2 * across + 1, 2 * ahead + 1, 2 * behind, 2 * ahead, 2 * behind + 1, 2 * chip, 2 * chip + 1)

    def span(t):
        return pl.ds(pl.multiple_of(t * CHUNK, CHUNK), CHUNK)

    def lanes_at(start, size=COLS):
        return pl.ds(pl.multiple_of(start, 128), size)

    def local_rows(j):
        return pltpu.make_async_copy(o_hbm.at[:, :, lanes_at(core * half + j * COLS)],
                                     pool.at[j, pl.ds(core * experts, experts)], rows_loc.at[j])

    def swap_rows(j):
        return pltpu.make_async_remote_copy(
            src_ref=o_hbm.at[:, :, lanes_at((1 - core) * half + j * COLS)], dst_ref=pool.at[j, pl.ds(core * experts, experts)],
            send_sem=rows_ss.at[j], recv_sem=rows_rs.at[j], device_id={'ep': partner}, device_id_type=MESH)

    local_resid = pltpu.make_async_copy(h_hbm.at[:, lanes_at(core * half, half)], resid_v.at[core], res_loc)
    swap_resid = pltpu.make_async_remote_copy(
        src_ref=h_hbm.at[:, lanes_at((1 - core) * half, half)], dst_ref=resid_v.at[core],
        send_sem=res_ss, recv_sem=res_rs, device_id={'ep': partner}, device_id_type=MESH)

    def meta_copy(step):
        return pltpu.make_async_remote_copy(
            src_ref=meta.at[me], dst_ref=meta.at[me], send_sem=meta_ss.at[step - 1], recv_sem=meta_rs.at[step - 1],
            device_id={'ep': (me + step) % ep}, device_id_type=MESH)

    def ring_copy(kind, s):
        target = right if kind % 2 == 0 else left
        return pltpu.make_async_remote_copy(
            src_ref=send_v.at[kind, s % 2], dst_ref=recv_v.at[kind, s], send_sem=ring_ss.at[kind, s],
            recv_sem=ring_rs.at[kind, s], device_id={'ep': target}, device_id_type=MESH)

    def y_copy(side, s):
        return pltpu.make_async_remote_copy(
            src_ref=ysend_v.at[side, s % 2], dst_ref=y_v.at[side, core * blocks + s % blocks, span(s // blocks)],
            send_sem=y_ss.at[side, s], recv_sem=y_rs.at[core, s],
            device_id={'pp': next_stage, 'ep': 2 * chip + side}, device_id_type=MESH)

    def y_relay(part, s):
        piece = y_v.at[core, part * blocks + s % blocks, span(s // blocks)]
        return pltpu.make_async_remote_copy(
            src_ref=piece, dst_ref=piece, send_sem=relay_ss.at[part, s], recv_sem=relay_rs.at[part, s],
            device_id={'ep': partner}, device_id_type=MESH)

    def mix_copy(pair, t):
        block = mix_v.at[core * pairs + pair, :, span(t)]
        return pltpu.make_async_remote_copy(
            src_ref=block, dst_ref=block, send_sem=mix_ss.at[t, pair], recv_sem=mix_rs.at[t, pair],
            device_id={'ep': partner}, device_id_type=MESH)

    def qkv_copies(which, pair, slot):
        w_hbm = (wq_hbm, wk_hbm, wv_hbm)[which]
        return [pltpu.make_async_copy(w_hbm.at[2 * (core * pairs + pair) + i],
                                      pool.at[slot, 0:depth, :, i * head_dim:(i + 1) * head_dim], w_sem.at[slot, i]) for i in range(2)]

    def out_copies(n):
        mid = depth // 2
        return [pltpu.make_async_copy(wo_hbm.at[i * mid:(i + 1) * mid, :, lanes_at(core * half + n * COLS)],
                                      pool.at[n, i * mid:(i + 1) * mid], w_sem.at[n, i]) for i in range(2)]

    def slot_of(unit):
        return blocks + unit % RING_SLOTS

    def start_all(copies):
        for copy in copies:
            copy.start()

    def wait_all(copies):
        for copy in copies:
            copy.wait()

    for j in range(blocks):
        local_rows(j).start()
    local_resid.start()
    kv_v[...] = jnp.zeros_like(kv_v)
    row_ids = jnp.where(slots[...] >= 0, ids[...] * cap_dev + slots[...] - me * cap_dev, -1)
    meta[me, 0:top, :] = row_ids.astype(jnp.float32)
    meta[me, top:2 * top, :] = gates[...]

    barrier = pltpu.get_barrier_semaphore()
    for step in range(1, ep):
        pl.semaphore_signal(barrier, inc=1, device_id={'ep': (me + step) % ep}, device_id_type=MESH)
    for side in range(2):
        pl.semaphore_signal(barrier, inc=1, device_id={'pp': next_stage, 'ep': 2 * chip + side}, device_id_type=MESH)
        pl.semaphore_signal(barrier, inc=1, device_id={'pp': prev_stage, 'ep': 2 * chip + side}, device_id_type=MESH)
    pl.semaphore_wait(barrier, ep - 1 + 4)

    for step in range(1, ep):
        meta_copy(step).start()
    for j in range(blocks):
        swap_rows(j).start()
    swap_resid.start()

    def build_gates(role):
        table = jnp.transpose(meta[owners[role]])
        wanted = (lax.broadcasted_iota(jnp.int32, (tokens, chip_rows), 1) + chip * chip_rows).astype(jnp.float32)
        total = jnp.zeros((tokens, chip_rows), jnp.float32)
        for t in range(top):
            total = total + jnp.where(table[:, t:t + 1] == wanted, table[:, top + t:top + t + 1], 0.0)
        high = total.astype(jnp.bfloat16)
        rest = total - high.astype(jnp.float32)
        mid = rest.astype(jnp.bfloat16)
        low = (rest - mid.astype(jnp.float32)).astype(jnp.bfloat16)
        for t in range(chunks):
            for i, term in enumerate((high, mid, low)):
                gate_mats[role, t, i * CHUNK:(i + 1) * CHUNK] = term[t * CHUNK:(t + 1) * CHUNK]

    def contribution(role, s):
        slot0 = pl.multiple_of(owners[role] * cap_dev, cap_dev)
        rows = pool[s % blocks, :, pl.ds(slot0, cap_dev), :].reshape(chip_rows, COLS)
        parts = jnp.dot(gate_mats[role, s // blocks], rows, preferred_element_type=jnp.float32)
        return parts[2 * CHUNK:] + parts[CHUNK:2 * CHUNK] + parts[:CHUNK]

    def leaf(kind, s):
        @pl.when(s >= 2)
        def _():
            ring_copy(kind, s - 2).wait_send()

        send_v[kind, s % 2] = contribution(kind, s)
        ring_copy(kind, s).start()

    def forward(kind, s):
        own = contribution(kind, s)

        @pl.when(s >= 2)
        def _():
            ring_copy(kind, s - 2).wait_send()

        ring_copy(kind - 4, s).wait_recv()
        send_v[kind, s % 2] = own + recv_v[kind - 4, s]
        ring_copy(kind, s).start()

    def finish(side, s):
        near, far = ((3, 4), (2, 5))[side]
        own = contribution(6 + side, s)

        @pl.when(s >= 2)
        def _():
            y_copy(side, s - 2).wait_send()

        ring_copy(near, s).wait_recv()
        ring_copy(far, s).wait_recv()
        resid = resid_v[side, span(s // blocks), lanes_at(s % blocks * COLS)].astype(jnp.float32)
        ysend_v[side, s % 2] = (resid + (own + recv_v[near, s] + recv_v[far, s])).astype(jnp.bfloat16)
        y_copy(side, s).start()

    def pass_on(s):
        for part in range(2):
            pltpu.make_async_copy(ysend_v.at[0, 0], ysend_v.at[0, 0], y_rs.at[part, s]).wait()
            y_relay(part, s).start()

    def take(s):
        @pl.when(s % blocks == 0)
        def _():
            square_v[...] = jnp.zeros_like(square_v)

        for part in range(2):
            y_relay(part, s).wait_recv()
            for seq in range(2):
                piece = y_v[seq, part * blocks + s % blocks, span(s // blocks)].astype(jnp.float32)
                square_v[seq] += piece * piece

    def normalize(t):
        for seq in range(2):
            mean = jnp.sum(square_v[seq], axis=-1, keepdims=True) / width
            inv_rms = lax.rsqrt(mean + NORM_EPS)
            for i in range(depth):
                cols = slice(i * COLS, (i + 1) * COLS)
                x_v[seq * CHUNK:(seq + 1) * CHUNK, cols] = (
                    y_v[seq, i, span(t)].astype(jnp.float32) * inv_rms * scale_ref[:, cols]).astype(jnp.bfloat16)

    def unit_of(which, pair, t):
        return (t * pairs + pair) * 3 + which

    def wait_pair(pair, t):
        for which in range(3):
            wait_all(qkv_copies(which, 0, slot_of(unit_of(which, pair, t))))

    def refill(pair, t):
        for which in range(3):
            unit = unit_of(which, pair, t) + RING_SLOTS

            @pl.when(unit < units)
            def _():
                start_all(qkv_copies((which + RING_SLOTS) % 3, unit // 3 % pairs, slot_of(unit)))

    def project(pair, t):
        for which in range(3):
            weight = pool[slot_of(unit_of(which, pair, t)), 0:depth].reshape(width, COLS)
            product = jnp.dot(x_v[...], weight, preferred_element_type=jnp.float32).astype(jnp.bfloat16)
            if which == 0:
                q_v[pair % 2] = product
            else:
                for seq in range(2):
                    kv_v[which - 1, pair, seq, span(t)] = product[seq * CHUNK:(seq + 1) * CHUNK]

    def attend(pair, t):
        causal = (lax.broadcasted_iota(jnp.int32, (CHUNK, tokens), 0) + t * CHUNK
                  >= lax.broadcasted_iota(jnp.int32, (CHUNK, tokens), 1))
        mixed = []
        for seq in range(2):
            for i in range(2):
                lanes = slice(i * head_dim, (i + 1) * head_dim)
                q = q_v[pair % 2, seq * CHUNK:(seq + 1) * CHUNK, lanes]
                k, v = kv_v[0, pair, seq, :, lanes], kv_v[1, pair, seq, :, lanes]
                scores = lax.dot_general(q, k, (((1,), (1,)), ((), ())), preferred_element_type=jnp.float32) * head_dim ** -0.5
                scores = jnp.where(causal, scores, -1e30)
                exps = jnp.exp(scores - jnp.max(scores, axis=-1, keepdims=True))
                sums = jnp.sum(exps, axis=-1, keepdims=True)
                mixed.append((jnp.dot(exps.astype(jnp.bfloat16), v, preferred_element_type=jnp.float32) / sums).astype(jnp.bfloat16))
        return mixed

    def store_mixed(pair, t, mixed):
        for seq in range(2):
            for i in range(2):
                mix_v[core * pairs + pair, seq, span(t), i * head_dim:(i + 1) * head_dim] = mixed[2 * seq + i]
        mix_copy(pair, t).start()

    for step in range(1, ep):
        meta_copy(step).wait_recv()

    def ring_step(s, carry):
        @pl.when(s < steps)
        def _():
            @pl.when(s < blocks)
            def _():
                local_rows(s).wait()
                swap_rows(s).wait_recv()

            for kind in range(4):
                @pl.when(s == 0)
                def _():
                    build_gates(kind)

                leaf(kind, s)

        @pl.when(s == 0)
        def _():
            for role in range(4, 8):
                build_gates(role)
            local_resid.wait()
            swap_resid.wait_recv()
            for unit in range(RING_SLOTS):
                start_all(qkv_copies(unit % 3, unit // 3, slot_of(unit)))

        @pl.when(jnp.logical_and(s >= 1, s < steps + 1))
        def _():
            forward(4, s - 1)
            forward(5, s - 1)

        @pl.when(jnp.logical_and(s >= 2, s < steps + 2))
        def _():
            finish(0, s - 2)
            finish(1, s - 2)

            @pl.when(s - 2 >= steps - blocks)
            def _():
                start_all(out_copies(s - 2 - (steps - blocks)))

        @pl.when(jnp.logical_and(s >= 3, s < steps + 3))
        def _():
            pass_on(s - 3)

        @pl.when(s >= 4)
        def _():
            take(s - 4)

        lag = s % blocks - 3

        @pl.when(jnp.logical_and(s >= blocks, lag == 0))
        def _():
            normalize(s // blocks - 1)

        @pl.when(jnp.logical_and(jnp.logical_and(s >= blocks, s < steps), lag >= 0))
        def _():
            def one_pair(pair, carry):
                t = s // blocks - 1
                wait_pair(pair, t)
                project(pair, t)
                store_mixed(pair, t, attend(pair, t))
                refill(pair, t)
                return carry

            lax.fori_loop(2 * lag, jnp.minimum(2 * lag + 2, pairs), one_pair, 0)
        return carry

    lax.fori_loop(0, steps + 4, ring_step, 0)

    last = chunks - 1
    wait_pair(0, last)
    project(0, last)
    refill(0, last)

    def pair_step(pair, carry):
        wait_pair(pair, last)
        mixed = attend(pair - 1, last)
        project(pair, last)
        store_mixed(pair - 1, last, mixed)
        refill(pair, last)
        return carry

    lax.fori_loop(1, pairs, pair_step, 0)
    store_mixed(pairs - 1, last, attend(pairs - 1, last))

    for t in range(chunks):
        for pair in range(pairs):
            mix_copy(pair, t).wait_recv()

    def store_z(n):
        return pltpu.make_async_copy(z_v.at[n % 2, core], z_out.at[:, lanes_at(core * half + n * COLS)], z_sem.at[n])

    def send_z(n):
        return pltpu.make_async_remote_copy(
            src_ref=z_v.at[n % 2, 1 - core], dst_ref=z_out.at[:, lanes_at(core * half + n * COLS)],
            send_sem=zr_ss.at[n], recv_sem=zr_rs.at[n], device_id={'ep': partner}, device_id_type=MESH)

    def out_step(n, carry):
        wait_all(out_copies(n))
        mixed = jnp.concatenate([mix_v[i].reshape(2 * tokens, COLS) for i in range(depth)], axis=1)
        weight = pool[n, 0:depth].reshape(width, COLS)
        product = jnp.dot(mixed, weight, preferred_element_type=jnp.float32).astype(jnp.bfloat16)

        @pl.when(n >= 2)
        def _():
            store_z(n - 2).wait()
            send_z(n - 2).wait_send()

        for seq in range(2):
            resid = y_v[seq, core * blocks + n].astype(jnp.float32)
            z_v[n % 2, seq] = (resid + product[seq * tokens:(seq + 1) * tokens].astype(jnp.float32)).astype(jnp.bfloat16)
        send_z(n).start()
        store_z(n).start()
        return carry

    lax.fori_loop(0, blocks, out_step, 0)
    for n in range(blocks - 2, blocks):
        store_z(n).wait()
        send_z(n).wait_send()
    for n in range(blocks):
        send_z(n).wait_recv()
    for step in range(1, ep):
        meta_copy(step).wait_send()
    for j in range(blocks):
        swap_rows(j).wait_send()
    swap_resid.wait_send()
    for t in range(chunks):
        for pair in range(pairs):
            mix_copy(pair, t).wait_send()
    for s in range(steps):
        for part in range(2):
            y_relay(part, s).wait_send()
    for s in range(steps - 2, steps):
        for kind in range(6):
            ring_copy(kind, s).wait_send()
        for side in range(2):
            y_copy(side, s).wait_send()


def combine_and_attend(ep, pp, expert_out, expert_ids, slot_ids, gate_vals, residual, norm_scale, w_query, w_key, w_value, w_out):
    experts, cap, width = expert_out.shape
    tokens, top = expert_ids.shape
    heads, head_dim = w_query.shape[1:]
    sizes = (ep, pp, experts, cap, width, tokens, top, heads, head_dim)
    half = width // 2
    blocks = half // COLS
    chunks = tokens // CHUNK
    steps = chunks * blocks
    depth = width // COLS
    pairs = heads // 4
    chip_rows = 2 * experts * cap // ep
    any_spec = pl.BlockSpec(memory_space=pl.ANY)
    vmem_spec = pl.BlockSpec(memory_space=pltpu.VMEM)
    dma = pltpu.SemaphoreType.DMA

    def by_head(weights):
        return jnp.swapaxes(weights, 0, 1).reshape(heads, depth, COLS, head_dim)

    return pl.pallas_call(
        functools.partial(layer_kernel, sizes),
        out_shape=jax.ShapeDtypeStruct((tokens, width), jnp.bfloat16),
        in_specs=[any_spec, vmem_spec, vmem_spec, vmem_spec, any_spec, vmem_spec] + [any_spec] * 4,
        out_specs=any_spec,
        scratch_shapes=[
            pltpu.VMEM((blocks + RING_SLOTS, 2 * experts, cap, COLS), jnp.bfloat16),
            pltpu.VMEM((2, tokens, half), jnp.bfloat16),
            pltpu.VMEM((ep, 2 * top, tokens), jnp.float32),
            pltpu.VMEM((8, chunks, 3 * CHUNK, chip_rows), jnp.bfloat16),
            pltpu.VMEM((6, 2, CHUNK, COLS), jnp.float32),
            pltpu.VMEM((6, steps, CHUNK, COLS), jnp.float32),
            pltpu.VMEM((2, 2, CHUNK, COLS), jnp.bfloat16),
            pltpu.VMEM((2, depth, tokens, COLS), jnp.bfloat16),
            pltpu.VMEM((2, CHUNK, COLS), jnp.float32),
            pltpu.VMEM((2 * CHUNK, width), jnp.bfloat16),
            pltpu.VMEM((2, 2 * CHUNK, COLS), jnp.bfloat16),
            pltpu.VMEM((2, pairs, 2, tokens, COLS), jnp.bfloat16),
            pltpu.VMEM((2 * pairs, 2, tokens, COLS), jnp.bfloat16),
            pltpu.VMEM((2, 2, tokens, COLS), jnp.bfloat16),
            dma((blocks,)), dma((blocks,)), dma((blocks,)), dma, dma, dma, dma((ep - 1,)), dma((ep - 1,)),
            dma((6, steps)), dma((6, steps)), dma((2, steps)), dma((2, steps)), dma((2, steps)), dma((2, steps)),
            dma((chunks, pairs)), dma((chunks, pairs)), dma((blocks + RING_SLOTS, 2)), dma((blocks,)), dma((blocks,)), dma((blocks,)),
        ],
        compiler_params=pltpu.CompilerParams(collective_id=0, has_side_effects=True, vmem_limit_bytes=67043328),
    )(expert_out, expert_ids.T, slot_ids.T, gate_vals.T, residual, norm_scale[None],
      by_head(w_query), by_head(w_key), by_head(w_value), w_out.reshape(depth, COLS, width))


def solution(mesh):
    ep_size = mesh.shape['ep']
    pp_size = mesh.shape['pp']
    token_spec = P(('data', 'pp'), 'ep', None, None)
    weight_spec = P('pp', None, None, None)

    def body(expert_out, expert_ids, slot_ids, gate_vals, residual, norm_scale, w_query, w_key, w_value, w_out):
        result = combine_and_attend(
            ep_size, pp_size, expert_out[0], expert_ids[0, 0], slot_ids[0, 0], gate_vals[0, 0], residual[0, 0],
            norm_scale[0], w_query[0], w_key[0], w_value[0], w_out[0])
        return result[None, None]

    return jax.shard_map(body, mesh=mesh, in_specs=(token_spec, token_spec, token_spec, token_spec, token_spec, P('pp', None), weight_spec, weight_spec, weight_spec, weight_spec), out_specs=token_spec, check_vma=False)
```

time: 172 us -> 151 us (0.88)
  matrix products: 53.9 us -> 0 us
  Pallas kernels: 113 us -> 149 us
  other arithmetic: 5.67 us -> 0 us
  local copies, waits for them, and re-layouts: 0.01 us -> 2.51 us
    dot_general x4 -> x0, matrix products: 53.9 us -> none  [the longest x1 17.7 us: attn_block(): jnp.einsum('crif,ife->cre', attn_out, w_out, preferred_element_type=jnp.f...]
    pallas_call x1, Pallas kernels: 113 us -> 149 us  [combine_and_attend(): pl.pallas_call(functools.partial(layer_kernel, sizes), out_shape=jax.Shap...]
    reduce_sum x2 -> x0, other arithmetic: 5.6 us -> none  [the longest x1 3.91 us: attn_block(): row_sums = jnp.sum(exp_scores, axis=-1)]
    unnamed x4 -> x1, local copies, waits for them, and re-layouts: 0.01 us -> 2.51 us
where the time goes in v3:
time: 151 us
  Pallas kernels  149 us (99%)
  local copies, waits for them, and re-layouts  2.51 us (2%)
    pallas_call x1, Pallas kernels, combine_and_attend(): pl.pallas_call(functools.partial(layer_kernel, sizes), out_shape=jax.Shap...  149 us

profile of v3, /device:TPU:97, one launch (start us, length us, event | category | flops | bytes accessed | tf_op | source)
XLA Modules:
  0.0 151.1 jit_solution(10564730925355354993)
XLA Ops:
  0.0 148.6 %shard_map.100 = bf16[192,3584]{1,0:T(8,128)(2,1)} custom-call(bf16[8,256,3584]{2,1,0:T(8,128)(2,1)} %bitcast.32, s32[8,192]{1,0:T(8,128)} %bitcast.35, s32[8,192]{1,0:T(8,128)} %bitcast.36, f32[8,192]{1,0:T(8,128)} %bitcast.37, bf16[192,3584]{1,0:T(8,128)(2,1)} %bitcast.34, f32[1,3584]{1,0:T(1,128)} %scale_ref.1, bf16[28,14,256,128]{3,2,1,0:T(8,128)(2,1)} %bitcast.28, ...), custom_call_target="tpu_custom_call" | custom-call | tf_op jit(solution)/shard_map/pallas_call | solution.py:417
  148.6 2.5 %copy.12 = bf16[1,1,192,3584]{3,2,1,0:T(8,128)(2,1)} copy(bf16[1,1,192,3584]{3,2,1,0:T(8,128)(2,1)} %bitcast.33) | data formatting | bytes 2752512

commit v4 on v3

--- a/solution.py
+++ b/solution.py
@@ -10,7 +10,7 @@
 NORM_EPS = 1e-6
 COLS = 256
 CHUNK = 96
-RING_SLOTS = 10
+RING_PAIRS = 3
 MESH = pl.DeviceIdType.MESH
 
 
@@ -28,7 +28,6 @@
     pairs = heads // 4
     cap_dev = cap // ep
     chip_rows = 2 * experts * cap_dev
-    units = chunks * pairs * 3
     me = lax.axis_index('ep')
     stage = lax.axis_index('pp')
     chip, core = me // 2, me % 2
@@ -97,8 +96,8 @@
         return [pltpu.make_async_copy(wo_hbm.at[i * mid:(i + 1) * mid, :, lanes_at(core * half + n * COLS)],
                                       pool.at[n, i * mid:(i + 1) * mid], w_sem.at[n, i]) for i in range(2)]
 
-    def slot_of(unit):
-        return blocks + unit % RING_SLOTS
+    def slot_of(which, pair):
+        return blocks + pair % RING_PAIRS * 3 + which
 
     def start_all(copies):
         for copy in copies:
@@ -111,7 +110,6 @@
     for j in range(blocks):
         local_rows(j).start()
     local_resid.start()
-    kv_v[...] = jnp.zeros_like(kv_v)
     row_ids = jnp.where(slots[...] >= 0, ids[...] * cap_dev + slots[...] - me * cap_dev, -1)
     meta[me, 0:top, :] = row_ids.astype(jnp.float32)
     meta[me, top:2 * top, :] = gates[...]
@@ -208,24 +206,27 @@
                 x_v[seq * CHUNK:(seq + 1) * CHUNK, cols] = (
                     y_v[seq, i, span(t)].astype(jnp.float32) * inv_rms * scale_ref[:, cols]).astype(jnp.bfloat16)
 
-    def unit_of(which, pair, t):
-        return (t * pairs + pair) * 3 + which
-
-    def wait_pair(pair, t):
+    def fetch(pair):
         for which in range(3):
-            wait_all(qkv_copies(which, 0, slot_of(unit_of(which, pair, t))))
+            start_all(qkv_copies(which, pair, slot_of(which, pair)))
+
+    def wait_pair(i, pair, t):
+        @pl.when(jnp.logical_or(t == 0, i >= RING_PAIRS))
+        def _():
+            for which in range(3):
+                wait_all(qkv_copies(which, 0, slot_of(which, pair)))
 
     def refill(pair, t):
-        for which in range(3):
-            unit = unit_of(which, pair, t) + RING_SLOTS
-
-            @pl.when(unit < units)
-            def _():
-                start_all(qkv_copies((which + RING_SLOTS) % 3, unit // 3 % pairs, slot_of(unit)))
+        odd = t % 2
+        later = pair + (1 - 2 * odd) * RING_PAIRS
+
+        @pl.when(jnp.logical_and(later >= 0, later < pairs))
+        def _():
+            fetch(later)
 
     def project(pair, t):
         for which in range(3):
-            weight = pool[slot_of(unit_of(which, pair, t)), 0:depth].reshape(width, COLS)
+            weight = pool[slot_of(which, pair), 0:depth].reshape(width, COLS)
             product = jnp.dot(x_v[...], weight, preferred_element_type=jnp.float32).astype(jnp.bfloat16)
             if which == 0:
                 q_v[pair % 2] = product
@@ -279,13 +280,33 @@
                 build_gates(role)
             local_resid.wait()
             swap_resid.wait_recv()
-            for unit in range(RING_SLOTS):
-                start_all(qkv_copies(unit % 3, unit // 3, slot_of(unit)))
+            kv_v[...] = jnp.zeros_like(kv_v)
+
+        for which in range(3):
+            @pl.when(jnp.logical_and(s % 3 == which, s < 3 * RING_PAIRS))
+            def _():
+                start_all(qkv_copies(which, s // 3, slot_of(which, s // 3)))
 
         @pl.when(jnp.logical_and(s >= 1, s < steps + 1))
         def _():
             forward(4, s - 1)
             forward(5, s - 1)
+
+        lag = s % blocks - 4
+
+        @pl.when(jnp.logical_and(jnp.logical_and(s >= blocks, s < steps), lag >= 0))
+        def _():
+            def one_pair(i, carry):
+                t = s // blocks - 1
+                odd = t % 2
+                pair = odd * (pairs - 1) + (1 - 2 * odd) * i
+                wait_pair(i, pair, t)
+                project(pair, t)
+                refill(pair, t)
+                store_mixed(pair, t, attend(pair, t))
+                return carry
+
+            lax.fori_loop(3 * lag, jnp.minimum(3 * lag + 3, pairs), one_pair, 0)
 
         @pl.when(jnp.logical_and(s >= 2, s < steps + 2))
         def _():
@@ -304,42 +325,34 @@
         def _():
             take(s - 4)
 
-        lag = s % blocks - 3
-
-        @pl.when(jnp.logical_and(s >= blocks, lag == 0))
+        @pl.when(jnp.logical_and(s >= blocks, s % blocks == 3))
         def _():
             normalize(s // blocks - 1)
 
-        @pl.when(jnp.logical_and(jnp.logical_and(s >= blocks, s < steps), lag >= 0))
-        def _():
-            def one_pair(pair, carry):
-                t = s // blocks - 1
-                wait_pair(pair, t)
-                project(pair, t)
-                store_mixed(pair, t, attend(pair, t))
-                refill(pair, t)
-                return carry
-
-            lax.fori_loop(2 * lag, jnp.minimum(2 * lag + 2, pairs), one_pair, 0)
         return carry
 
     lax.fori_loop(0, steps + 4, ring_step, 0)
 
     last = chunks - 1
-    wait_pair(0, last)
-    project(0, last)
-    refill(0, last)
-
-    def pair_step(pair, carry):
-        wait_pair(pair, last)
-        mixed = attend(pair - 1, last)
-        project(pair, last)
-        store_mixed(pair - 1, last, mixed)
-        refill(pair, last)
+    flip = last % 2
+
+    def nth(i):
+        return pairs - 1 - i if flip else i
+
+    wait_pair(0, nth(0), last)
+    project(nth(0), last)
+    refill(nth(0), last)
+
+    def pair_step(i, carry):
+        wait_pair(i, nth(i), last)
+        mixed = attend(nth(i - 1), last)
+        project(nth(i), last)
+        store_mixed(nth(i - 1), last, mixed)
+        refill(nth(i), last)
         return carry
 
     lax.fori_loop(1, pairs, pair_step, 0)
-    store_mixed(pairs - 1, last, attend(pairs - 1, last))
+    store_mixed(nth(pairs - 1), last, attend(nth(pairs - 1), last))
 
     for t in range(chunks):
         for pair in range(pairs):
@@ -420,7 +433,7 @@
         in_specs=[any_spec, vmem_spec, vmem_spec, vmem_spec, any_spec, vmem_spec] + [any_spec] * 4,
         out_specs=any_spec,
         scratch_shapes=[
-            pltpu.VMEM((blocks + RING_SLOTS, 2 * experts, cap, COLS), jnp.bfloat16),
+            pltpu.VMEM((blocks + 3 * RING_PAIRS, 2 * experts, cap, COLS), jnp.bfloat16),
             pltpu.VMEM((2, tokens, half), jnp.bfloat16),
             pltpu.VMEM((ep, 2 * top, tokens), jnp.float32),
             pltpu.VMEM((8, chunks, 3 * CHUNK, chip_rows), jnp.bfloat16),
@@ -436,7 +449,7 @@
             pltpu.VMEM((2, 2, tokens, COLS), jnp.bfloat16),
             dma((blocks,)), dma((blocks,)), dma((blocks,)), dma, dma, dma, dma((ep - 1,)), dma((ep - 1,)),
             dma((6, steps)), dma((6, steps)), dma((2, steps)), dma((2, steps)), dma((2, steps)), dma((2, steps)),
-            dma((chunks, pairs)), dma((chunks, pairs)), dma((blocks + RING_SLOTS, 2)), dma((blocks,)), dma((blocks,)), dma((blocks,)),
+            dma((chunks, pairs)), dma((chunks, pairs)), dma((blocks + 3 * RING_PAIRS, 2)), dma((blocks,)), dma((blocks,)), dma((blocks,)),
         ],
         compiler_params=pltpu.CompilerParams(collective_id=0, has_side_effects=True, vmem_limit_bytes=67043328),
     )(expert_out, expert_ids.T, slot_ids.T, gate_vals.T, residual, norm_scale[None],

time: 151 us -> 150 us (level)
  no operation moved by 1% of the time
where the time goes in v4:
time: 150 us
  Pallas kernels  148 us (99%)
  local copies, waits for them, and re-layouts  2.51 us (2%)
    pallas_call x1, Pallas kernels, combine_and_attend(): pl.pallas_call(functools.partial(layer_kernel, sizes), out_shape=jax.Shap...  148 us

profile of v4, /device:TPU:97, one launch (start us, length us, event | category | flops | bytes accessed | tf_op | source)
XLA Modules:
  0.0 150.3 jit_solution(14296022201974432025)
XLA Ops:
  0.0 147.8 %shard_map.100 = bf16[192,3584]{1,0:T(8,128)(2,1)} custom-call(bf16[8,256,3584]{2,1,0:T(8,128)(2,1)} %bitcast.32, s32[8,192]{1,0:T(8,128)} %bitcast.35, s32[8,192]{1,0:T(8,128)} %bitcast.36, f32[8,192]{1,0:T(8,128)} %bitcast.37, bf16[192,3584]{1,0:T(8,128)(2,1)} %bitcast.34, f32[1,3584]{1,0:T(1,128)} %scale_ref.1, bf16[28,14,256,128]{3,2,1,0:T(8,128)(2,1)} %bitcast.28, ...), custom_call_target="tpu_custom_call" | custom-call | tf_op jit(solution)/shard_map/pallas_call | solution.py:430
  147.8 2.5 %copy.12 = bf16[1,1,192,3584]{3,2,1,0:T(8,128)(2,1)} copy(bf16[1,1,192,3584]{3,2,1,0:T(8,128)(2,1)} %bitcast.33) | data formatting | bytes 2752512

commit v5 on v4

--- a/solution.py
+++ b/solution.py
@@ -9,7 +9,7 @@
 
 NORM_EPS = 1e-6
 COLS = 256
-CHUNK = 96
+CHUNK = 192
 RING_PAIRS = 3
 MESH = pl.DeviceIdType.MESH
 

time: 150 us -> 147 us (0.980)
  Pallas kernels: 148 us -> 144 us
    pallas_call x1, Pallas kernels: 148 us -> 144 us  [combine_and_attend(): pl.pallas_call(functools.partial(layer_kernel, sizes), out_shape=jax.Shap...]
where the time goes in v5:
time: 147 us
  Pallas kernels  144 us (98%)
  local copies, waits for them, and re-layouts  2.51 us (2%)
    pallas_call x1, Pallas kernels, combine_and_attend(): pl.pallas_call(functools.partial(layer_kernel, sizes), out_shape=jax.Shap...  144 us

profile of v5, /device:TPU:97, one launch (start us, length us, event | category | flops | bytes accessed | tf_op | source)
XLA Modules:
  0.0 146.9 jit_solution(2327518921719813327)
XLA Ops:
  0.0 144.4 %shard_map.100 = bf16[192,3584]{1,0:T(8,128)(2,1)} custom-call(bf16[8,256,3584]{2,1,0:T(8,128)(2,1)} %bitcast.32, s32[8,192]{1,0:T(8,128)} %bitcast.35, s32[8,192]{1,0:T(8,128)} %bitcast.36, f32[8,192]{1,0:T(8,128)} %bitcast.37, bf16[192,3584]{1,0:T(8,128)(2,1)} %bitcast.34, f32[1,3584]{1,0:T(1,128)} %scale_ref.1, bf16[28,14,256,128]{3,2,1,0:T(8,128)(2,1)} %bitcast.28, ...), custom_call_target="tpu_custom_call" | custom-call | tf_op jit(solution)/shard_map/pallas_call | solution.py:430
  144.4 2.5 %copy.12 = bf16[1,1,192,3584]{3,2,1,0:T(8,128)(2,1)} copy(bf16[1,1,192,3584]{3,2,1,0:T(8,128)(2,1)} %bitcast.33) | data formatting | bytes 2752512

commit v6 on v5

--- a/solution.py
+++ b/solution.py
@@ -107,9 +107,7 @@
         for copy in copies:
             copy.wait()
 
-    for j in range(blocks):
-        local_rows(j).start()
-    local_resid.start()
+    local_rows(0).start()
     row_ids = jnp.where(slots[...] >= 0, ids[...] * cap_dev + slots[...] - me * cap_dev, -1)
     meta[me, 0:top, :] = row_ids.astype(jnp.float32)
     meta[me, top:2 * top, :] = gates[...]
@@ -124,8 +122,11 @@
 
     for step in range(1, ep):
         meta_copy(step).start()
-    for j in range(blocks):
+    swap_rows(0).start()
+    for j in range(1, blocks):
+        local_rows(j).start()
         swap_rows(j).start()
+    local_resid.start()
     swap_resid.start()
 
     def build_gates(role):
@@ -282,40 +283,20 @@
             swap_resid.wait_recv()
             kv_v[...] = jnp.zeros_like(kv_v)
 
-        for which in range(3):
-            @pl.when(jnp.logical_and(s % 3 == which, s < 3 * RING_PAIRS))
-            def _():
-                start_all(qkv_copies(which, s // 3, slot_of(which, s // 3)))
-
         @pl.when(jnp.logical_and(s >= 1, s < steps + 1))
         def _():
             forward(4, s - 1)
             forward(5, s - 1)
 
-        lag = s % blocks - 4
-
-        @pl.when(jnp.logical_and(jnp.logical_and(s >= blocks, s < steps), lag >= 0))
-        def _():
-            def one_pair(i, carry):
-                t = s // blocks - 1
-                odd = t % 2
-                pair = odd * (pairs - 1) + (1 - 2 * odd) * i
-                wait_pair(i, pair, t)
-                project(pair, t)
-                refill(pair, t)
-                store_mixed(pair, t, attend(pair, t))
-                return carry
-
-            lax.fori_loop(3 * lag, jnp.minimum(3 * lag + 3, pairs), one_pair, 0)
-
         @pl.when(jnp.logical_and(s >= 2, s < steps + 2))
         def _():
             finish(0, s - 2)
             finish(1, s - 2)
 
-            @pl.when(s - 2 >= steps - blocks)
+            @pl.when(s - 2 == steps - 1)
             def _():
-                start_all(out_copies(s - 2 - (steps - blocks)))
+                fetch(0)
+                fetch(1)
 
         @pl.when(jnp.logical_and(s >= 3, s < steps + 3))
         def _():
@@ -333,6 +314,8 @@
 
     lax.fori_loop(0, steps + 4, ring_step, 0)
 
+    for pair in range(2, RING_PAIRS):
+        fetch(pair)
     last = chunks - 1
     flip = last % 2
 
@@ -342,6 +325,7 @@
     wait_pair(0, nth(0), last)
     project(nth(0), last)
     refill(nth(0), last)
+    start_all(out_copies(0))
 
     def pair_step(i, carry):
         wait_pair(i, nth(i), last)
@@ -349,6 +333,7 @@
         project(nth(i), last)
         store_mixed(nth(i - 1), last, mixed)
         refill(nth(i), last)
+        start_all(out_copies(i))
         return carry
 
     lax.fori_loop(1, pairs, pair_step, 0)

time: 147 us -> 147 us (level)
  no operation moved by 1% of the time
where the time goes in v6:
time: 147 us
  Pallas kernels  144 us (98%)
  local copies, waits for them, and re-layouts  2.51 us (2%)
    pallas_call x1, Pallas kernels, combine_and_attend(): pl.pallas_call(functools.partial(layer_kernel, sizes), out_shape=jax.Shap...  144 us

profile of v6, /device:TPU:97, one launch (start us, length us, event | category | flops | bytes accessed | tf_op | source)
XLA Modules:
  0.0 146.7 jit_solution(1493245672443276545)
XLA Ops:
  0.0 144.1 %shard_map.100 = bf16[192,3584]{1,0:T(8,128)(2,1)} custom-call(bf16[8,256,3584]{2,1,0:T(8,128)(2,1)} %bitcast.32, s32[8,192]{1,0:T(8,128)} %bitcast.35, s32[8,192]{1,0:T(8,128)} %bitcast.36, f32[8,192]{1,0:T(8,128)} %bitcast.37, bf16[192,3584]{1,0:T(8,128)(2,1)} %bitcast.34, f32[1,3584]{1,0:T(1,128)} %scale_ref.1, bf16[28,14,256,128]{3,2,1,0:T(8,128)(2,1)} %bitcast.28, ...), custom_call_target="tpu_custom_call" | custom-call | tf_op jit(solution)/shard_map/pallas_call | solution.py:415
  144.1 2.5 %copy.12 = bf16[1,1,192,3584]{3,2,1,0:T(8,128)(2,1)} copy(bf16[1,1,192,3584]{3,2,1,0:T(8,128)(2,1)} %bitcast.33) | data formatting | bytes 2752512

commit v7 on v4

--- a/solution.py
+++ b/solution.py
@@ -10,14 +10,14 @@
 NORM_EPS = 1e-6
 COLS = 256
 CHUNK = 96
-RING_PAIRS = 3
+RING_PAIRS = 4
 MESH = pl.DeviceIdType.MESH
 
 
 def layer_kernel(sizes, o_hbm, ids, slots, gates, h_hbm, scale_ref, wq_hbm, wk_hbm, wv_hbm, wo_hbm, z_out,
-                 pool, resid_v, meta, gate_mats, send_v, recv_v, ysend_v, y_v, square_v, x_v, q_v, kv_v, mix_v, z_v,
+                 pool, heads_v, resid_v, meta, gate_mats, send_v, recv_v, ysend_v, y_v, square_v, x_v, q_v, kv_v, mix_v, z_v,
                  rows_loc, rows_ss, rows_rs, res_loc, res_ss, res_rs, meta_ss, meta_rs,
-                 ring_ss, ring_rs, y_ss, y_rs, relay_ss, relay_rs, mix_ss, mix_rs, w_sem, z_sem, zr_ss, zr_rs):
+                 ring_ss, ring_rs, y_ss, y_rs, relay_ss, relay_rs, mix_ss, mix_rs, qkv_sem, w_sem, z_sem, zr_ss, zr_rs):
     ep, pp, experts, cap, width, tokens, top, heads, head_dim = sizes
     chips = ep // 2
     half = width // 2
@@ -89,7 +89,7 @@
     def qkv_copies(which, pair, slot):
         w_hbm = (wq_hbm, wk_hbm, wv_hbm)[which]
         return [pltpu.make_async_copy(w_hbm.at[2 * (core * pairs + pair) + i],
-                                      pool.at[slot, 0:depth, :, i * head_dim:(i + 1) * head_dim], w_sem.at[slot, i]) for i in range(2)]
+                                      heads_v.at[slot, i], qkv_sem.at[slot, i]) for i in range(2)]
 
     def out_copies(n):
         mid = depth // 2
@@ -97,7 +97,7 @@
                                       pool.at[n, i * mid:(i + 1) * mid], w_sem.at[n, i]) for i in range(2)]
 
     def slot_of(which, pair):
-        return blocks + pair % RING_PAIRS * 3 + which
+        return pair % RING_PAIRS * 3 + which
 
     def start_all(copies):
         for copy in copies:
@@ -226,7 +226,8 @@
 
     def project(pair, t):
         for which in range(3):
-            weight = pool[slot_of(which, pair), 0:depth].reshape(width, COLS)
+            slot = slot_of(which, pair)
+            weight = jnp.concatenate([heads_v[slot, i].reshape(width, head_dim) for i in range(2)], axis=1)
             product = jnp.dot(x_v[...], weight, preferred_element_type=jnp.float32).astype(jnp.bfloat16)
             if which == 0:
                 q_v[pair % 2] = product
@@ -433,7 +434,8 @@
         in_specs=[any_spec, vmem_spec, vmem_spec, vmem_spec, any_spec, vmem_spec] + [any_spec] * 4,
         out_specs=any_spec,
         scratch_shapes=[
-            pltpu.VMEM((blocks + 3 * RING_PAIRS, 2 * experts, cap, COLS), jnp.bfloat16),
+            pltpu.VMEM((blocks, 2 * experts, cap, COLS), jnp.bfloat16),
+            pltpu.VMEM((3 * RING_PAIRS, 2, depth, COLS, head_dim), jnp.bfloat16),
             pltpu.VMEM((2, tokens, half), jnp.bfloat16),
             pltpu.VMEM((ep, 2 * top, tokens), jnp.float32),
             pltpu.VMEM((8, chunks, 3 * CHUNK, chip_rows), jnp.bfloat16),
@@ -449,7 +451,7 @@
             pltpu.VMEM((2, 2, tokens, COLS), jnp.bfloat16),
             dma((blocks,)), dma((blocks,)), dma((blocks,)), dma, dma, dma, dma((ep - 1,)), dma((ep - 1,)),
             dma((6, steps)), dma((6, steps)), dma((2, steps)), dma((2, steps)), dma((2, steps)), dma((2, steps)),
-            dma((chunks, pairs)), dma((chunks, pairs)), dma((blocks + 3 * RING_PAIRS, 2)), dma((blocks,)), dma((blocks,)), dma((blocks,)),
+            dma((chunks, pairs)), dma((chunks, pairs)), dma((3 * RING_PAIRS, 2)), dma((blocks, 2)), dma((blocks,)), dma((blocks,)), dma((blocks,)),
         ],
         compiler_params=pltpu.CompilerParams(collective_id=0, has_side_effects=True, vmem_limit_bytes=67043328),
     )(expert_out, expert_ids.T, slot_ids.T, gate_vals.T, residual, norm_scale[None],

time: 150 us -> 150 us (level)
  no operation moved by 1% of the time
where the time goes in v7:
time: 150 us
  Pallas kernels  148 us (99%)
  local copies, waits for them, and re-layouts  2.51 us (2%)
    pallas_call x1, Pallas kernels, combine_and_attend(): pl.pallas_call(functools.partial(layer_kernel, sizes), out_shape=jax.Shap...  148 us

profile of v7, /device:TPU:97, one launch (start us, length us, event | category | flops | bytes accessed | tf_op | source)
XLA Modules:
  0.0 150.3 jit_solution(18131993773049225020)
XLA Ops:
  0.0 147.7 %shard_map.100 = bf16[192,3584]{1,0:T(8,128)(2,1)} custom-call(bf16[8,256,3584]{2,1,0:T(8,128)(2,1)} %bitcast.32, s32[8,192]{1,0:T(8,128)} %bitcast.35, s32[8,192]{1,0:T(8,128)} %bitcast.36, f32[8,192]{1,0:T(8,128)} %bitcast.37, bf16[192,3584]{1,0:T(8,128)(2,1)} %bitcast.34, f32[1,3584]{1,0:T(1,128)} %scale_ref.1, bf16[28,14,256,128]{3,2,1,0:T(8,128)(2,1)} %bitcast.28, ...), custom_call_target="tpu_custom_call" | custom-call | tf_op jit(solution)/shard_map/pallas_call | solution.py:431
  147.7 2.5 %copy.12 = bf16[1,1,192,3584]{3,2,1,0:T(8,128)(2,1)} copy(bf16[1,1,192,3584]{3,2,1,0:T(8,128)(2,1)} %bitcast.33) | data formatting | bytes 2752512

commit v8 on v2

--- a/solution.py
+++ b/solution.py
@@ -13,10 +13,10 @@
 MESH = pl.DeviceIdType.MESH
 
 
-def layer_kernel(sizes, o_hbm, ids, slots, gates, h_hbm, scale_ref, wq_hbm, wk_hbm, wv_hbm, wo_hbm, z_out,
+def layer_kernel(sizes, o_hbm, ids, slots, gates, h_hbm, scale_ref, wq_hbm, wk_hbm, wv_hbm, wo_hbm, z_out, y_out,
                  pool, resid_v, meta, gate_mats, send_v, recv_v, ysend_v, y_v, square_v, x_v, qkv_v, mix_v, z_v,
                  rows_loc, rows_ss, rows_rs, res_loc, res_ss, res_rs, meta_ss, meta_rs,
-                 ring_ss, ring_rs, y_ss, y_rs, w_sem, z_sem):
+                 ring_ss, ring_rs, y_ss, y_rs, w_sem, z_sem, yo_sem):
     ep, pp, experts, cap, width, tokens, top, heads, head_dim = sizes
     chips = ep // 2
     half = width // 2
@@ -54,17 +54,20 @@
             src_ref=meta.at[me], dst_ref=meta.at[me], send_sem=meta_ss.at[step - 1], recv_sem=meta_rs.at[step - 1],
             device_id={'ep': (me + step) % ep}, device_id_type=MESH)
 
-    def ring_copy(kind, j):
+    def part(hf):
+        return slice(hf * tokens // 2, (hf + 1) * tokens // 2)
+
+    def ring_copy(kind, j, hf=0):
         target = right if kind % 2 == 0 else left
+        rows = part(hf) if kind >= 4 else slice(0, tokens)
         return pltpu.make_async_remote_copy(
-            src_ref=send_v.at[kind, j % 2], dst_ref=recv_v.at[kind, j], send_sem=ring_ss.at[kind, j],
-            recv_sem=ring_rs.at[kind, j], device_id={'ep': target}, device_id_type=MESH)
-
-    def y_copy(side, j):
+            src_ref=send_v.at[kind, j % 2, rows], dst_ref=recv_v.at[kind, j, rows], send_sem=ring_ss.at[kind + 2 * hf, j],
+            recv_sem=ring_rs.at[kind + 2 * hf, j], device_id={'ep': target}, device_id_type=MESH)
+
+    def y_copy(side, j, hf):
         return pltpu.make_async_remote_copy(
-            src_ref=ysend_v.at[side, j % 2], dst_ref=y_v.at[core * blocks + j], send_sem=y_ss.at[side, j],
-            recv_sem=y_rs.at[core * blocks + j], device_id={'pp': next_stage, 'ep': 2 * chip + side}, device_id_type=MESH)
-
+            src_ref=ysend_v.at[side, j % 2, part(hf)], dst_ref=y_v.at[core * blocks + j, part(hf)], send_sem=y_ss.at[hf, side, j],
+            recv_sem=y_rs.at[hf, core * blocks + j], device_id={'pp': next_stage, 'ep': 2 * chip + side}, device_id_type=MESH)
 
     pairs = heads // 2
     depth = width // COLS
@@ -110,9 +113,15 @@
             piece = y_v[side * blocks + j].astype(jnp.float32)
             square_v[...] += piece * piece
 
+    def store_y(i):
+        return pltpu.make_async_copy(y_v.at[i], y_out.at[:, pl.ds(pl.multiple_of(i * COLS, COLS), COLS)], yo_sem.at[i])
+
     def wait_y(j):
         for side in range(2):
-            pltpu.make_async_copy(y_v.at[side * blocks + j], y_v.at[side * blocks + j], y_rs.at[side * blocks + j]).wait()
+            for hf in range(2):
+                piece = y_v.at[side * blocks + j, part(hf)]
+                pltpu.make_async_copy(piece, piece, y_rs.at[hf, side * blocks + j]).wait()
+            store_y(side * blocks + j).start()
 
     for j in range(blocks):
         local_rows(j).start()
@@ -157,19 +166,24 @@
         return parts[2 * tokens:] + parts[tokens:2 * tokens] + parts[:tokens]
 
     def finish(j):
-        for side, (near, far) in enumerate(((3, 4), (2, 5))):
-            own = contribution(6 + side, j)
-
-            @pl.when(j >= 2)
-            def _():
-                y_copy(side, j - 2).wait_send()
-
-            ring_copy(near, j).wait_recv()
-            ring_copy(far, j).wait_recv()
-            cols = pl.ds(pl.multiple_of(j * COLS, COLS), COLS)
-            total = resid_v[side, :, cols].astype(jnp.float32) + (own + recv_v[near, j] + recv_v[far, j])
-            ysend_v[side, j % 2] = total.astype(jnp.bfloat16)
-            y_copy(side, j).start()
+        cols = pl.ds(pl.multiple_of(j * COLS, COLS), COLS)
+        owns = [contribution(6 + side, j) for side in range(2)]
+
+        @pl.when(j >= 2)
+        def _():
+            for side in range(2):
+                for hf in range(2):
+                    y_copy(side, j - 2, hf).wait_send()
+
+        for hf in range(2):
+            for side, (near, far) in enumerate(((3, 4), (2, 5))):
+                if hf == 0:
+                    ring_copy(near, j).wait_recv()
+                ring_copy(far, j, hf).wait_recv()
+                resid = resid_v[side, part(hf), cols].astype(jnp.float32)
+                total = resid + (owns[side][part(hf)] + recv_v[near, j, part(hf)] + recv_v[far, j, part(hf)])
+                ysend_v[side, j % 2, part(hf)] = total.astype(jnp.bfloat16)
+                y_copy(side, j, hf).start()
 
     for step in range(1, ep):
         meta_copy(step).wait_recv()
@@ -214,11 +228,13 @@
 
             @pl.when(j >= 2)
             def _():
-                ring_copy(kind, j - 2).wait_send()
+                for hf in range(2):
+                    ring_copy(kind, j - 2, hf).wait_send()
 
             ring_copy(kind - 4, j).wait_recv()
             send_v[kind, j % 2] = own + recv_v[kind - 4, j]
-            ring_copy(kind, j).start()
+            for hf in range(2):
+                ring_copy(kind, j, hf).start()
         return carry
 
     lax.fori_loop(0, blocks, block_step, 0)
@@ -298,7 +314,7 @@
         def _():
             store_z(n - 2).wait()
 
-        z_v[n % 2] = (y_v[n].astype(jnp.float32) + product.astype(jnp.float32)).astype(jnp.bfloat16)
+        z_v[n % 2] = product
         store_z(n).start()
         start_unit(3 * pairs + n + n_slots, 0)
         return carry
@@ -306,16 +322,20 @@
     lax.fori_loop(0, depth, out_step, 0)
     store_z(depth - 2).wait()
     store_z(depth - 1).wait()
+    for i in range(depth):
+        store_y(i).wait()
     for step in range(1, ep):
         meta_copy(step).wait_send()
     for j in range(blocks):
         swap_rows(j).wait_send()
     swap_resid.wait_send()
     for j in range(blocks - 2, blocks):
-        for kind in range(6):
+        for kind in range(4):
             ring_copy(kind, j).wait_send()
-        for side in range(2):
-            y_copy(side, j).wait_send()
+        for hf in range(2):
+            for side in range(2):
+                ring_copy(4 + side, j, hf).wait_send()
+                y_copy(side, j, hf).wait_send()
 
 
 def combine_and_attend(ep, pp, expert_out, expert_ids, slot_ids, gate_vals, residual, norm_scale, w_query, w_key, w_value, w_out):
@@ -335,9 +355,9 @@
 
     return pl.pallas_call(
         functools.partial(layer_kernel, sizes),
-        out_shape=jax.ShapeDtypeStruct((tokens, width), jnp.bfloat16),
+        out_shape=[jax.ShapeDtypeStruct((tokens, width), jnp.bfloat16)] * 2,
         in_specs=[any_spec, vmem_spec, vmem_spec, vmem_spec, any_spec, vmem_spec] + [any_spec] * 4,
-        out_specs=any_spec,
+        out_specs=[any_spec, any_spec],
         scratch_shapes=[
             pltpu.VMEM((SLOTS, 2 * experts, cap, COLS), jnp.bfloat16),
             pltpu.VMEM((2, tokens, width // 2), jnp.bfloat16),
@@ -353,7 +373,7 @@
             pltpu.VMEM((tokens, heads * head_dim), jnp.bfloat16),
             pltpu.VMEM((2, tokens, COLS), jnp.bfloat16),
             dma((blocks,)), dma((blocks,)), dma((blocks,)), dma, dma, dma, dma((ep - 1,)), dma((ep - 1,)),
-            dma((6, blocks)), dma((6, blocks)), dma((2, blocks)), dma((2 * blocks,)), dma((SLOTS, 2)), dma((2,)),
+            dma((8, blocks)), dma((8, blocks)), dma((2, 2, blocks)), dma((2, 2 * blocks)), dma((SLOTS, 2)), dma((2,)), dma((depth,)),
         ],
         compiler_params=pltpu.CompilerParams(collective_id=0, has_side_effects=True, vmem_limit_bytes=67043328),
     )(expert_out, expert_ids.T, slot_ids.T, gate_vals.T, residual, norm_scale[None],
@@ -367,9 +387,10 @@
     weight_spec = P('pp', None, None, None)
 
     def body(expert_out, expert_ids, slot_ids, gate_vals, residual, norm_scale, w_query, w_key, w_value, w_out):
-        result = combine_and_attend(
+        projected, arrived = combine_and_attend(
             ep_size, pp_size, expert_out[0], expert_ids[0, 0], slot_ids[0, 0], gate_vals[0, 0], residual[0, 0],
             norm_scale[0], w_query[0], w_key[0], w_value[0], w_out[0])
+        result = (arrived.astype(jnp.float32) + projected.astype(jnp.float32)).astype(jnp.bfloat16)
         return result[None, None]
 
     return jax.shard_map(body, mesh=mesh, in_specs=(token_spec, token_spec, token_spec, token_spec, token_spec, P('pp', None), weight_spec, weight_spec, weight_spec, weight_spec), out_specs=token_spec, check_vma=False)

time: 147 us -> 147 us (level)
  other arithmetic: 0 us -> 3.15 us
  local copies, waits for them, and re-layouts: 2.51 us -> 0 us
    broadcast_in_dim x0 -> x1, other arithmetic: none -> 3.15 us  [body(): return result[None, None]]
    unnamed x1 -> x0, local copies, waits for them, and re-layouts: 2.51 us -> none
where the time goes in v8:
time: 147 us; the launch traced here: 146 us
  Pallas kernels  143 us (97%)
  other arithmetic  3.15 us (2%)
    pallas_call x1, Pallas kernels, combine_and_attend(): pl.pallas_call(functools.partial(layer_kernel, sizes), out_shape=[jax.Sha...  143 us
    broadcast_in_dim x1, other arithmetic, body(): return result[None, None]  3.15 us

profile of v8, /device:TPU:97, one launch (start us, length us, event | category | flops | bytes accessed | tf_op | source)
XLA Modules:
  0.0 146.4 jit_solution(6287477493264186382)
XLA Ops:
  0.0 143.2 %shard_map.100 = (bf16[192,3584]{1,0:T(8,128)(2,1)}, bf16[192,3584]{1,0:T(8,128)(2,1)}) custom-call(bf16[8,256,3584]{2,1,0:T(8,128)(2,1)} %bitcast.33, s32[8,192]{1,0:T(8,128)} %bitcast.35, s32[8,192]{1,0:T(8,128)} %bitcast.36, f32[8,192]{1,0:T(8,128)} %bitcast.37, bf16[192,3584]{1,0:T(8,128)(2,1)} %bitcast.34, f32[1,3584]{1,0:T(1,128)} %scale_ref.1, ...), custom_call_target="tpu_custom_call" | custom-call | tf_op jit(solution)/shard_map/pallas_call | solution.py:356
  143.3 3.1 %fusion = bf16[1,1,192,3584]{3,2,1,0:T(8,128)(2,1)} fusion(bf16[192,3584]{1,0:T(8,128)(2,1)} %get-tuple-element.8, bf16[192,3584]{1,0:T(8,128)(2,1)} %get-tuple-element.7), kind=kLoop, calls=%fused_computation.1 | loop fusion | flops 2752512 | bytes 4128768 | tf_op jit(solution)/shard_map/broadcast_in_dim | solution.py:394
